TPU v7x, 32 devices: a whole 2x2x4 slice. The times are simulated.
32 devices in a mesh: rep: 4 (over y, core), tp: 8 (over z, x).
Axes of the slice: x: 2, y: 2, z: 4, core: 2. Of those that a mesh axis runs over, the one named last changes fastest.
Arguments:
- activations: bfloat16 [4, 2048, 4096], P('rep', 'tp'), may hold values from -6 to 6
- cotangent: bfloat16 [4, 2048, 8192], P('rep', None, 'tp'), may hold values from -0.13183594 to 0.13183594
- drift: bfloat16 [4, 4096, 8192], P('rep', None, 'tp'), may hold values from -8 to 8
- outer_weights: float32 [4096, 8192], P(('rep', 'tp')), may hold values from -6 to 6
- momentum: float32 [4096, 8192], P(('rep', 'tp')), may hold values from -6 to 6
Outputs:
- weights: bfloat16 [4096, 8192], P(None, 'tp')
- new_outer: float32 [4096, 8192], P(('rep', 'tp'))
- new_momentum: float32 [4096, 8192], P(('rep', 'tp'))
All inputs are finite; a program needn't handle non-finite values.
Results may differ from a plain program's by a relative error of at most 0.0085.
Values may be sent and summed in bfloat16 or wider, within the bound.
No kernel may reach another device: no remote copies, remote signals or barrier semaphores. Data moves between devices by JAX's collectives and lax.ppermute only.
A program may use at most 128 MiB of HBM per device.

v0:
```python
import jax
import jax.numpy as jnp
from jax import lax
from jax.sharding import PartitionSpec as P

outer_rate = 0.7
nesterov = 0.9


def on_device(activations, cotangent, drift, outer_weights, momentum):
    replicas = lax.axis_size("rep")
    cot_rows = cotangent[0]
    width = activations.shape[2]
    local_cols = cot_rows.shape[1]
    flat_rows = outer_weights.shape[0]
    grad = jnp.einsum(
        "td,tf->df",
        lax.all_gather(activations, "tp", axis=1, tiled=True)[0],
        cot_rows,
        preferred_element_type=jnp.float32,
    )
    delta = lax.optimization_barrier((drift[0].astype(jnp.float32) + grad).astype(jnp.bfloat16))
    summed = lax.psum_scatter(
        delta.astype(jnp.float32).astype(jnp.bfloat16), "rep", scatter_dimension=0, tiled=True
    ).astype(jnp.float32)
    summed = lax.all_to_all(
        summed.astype(jnp.bfloat16), "tp", split_axis=0, concat_axis=1, tiled=True
    ).astype(summed.dtype)
    average = summed / replicas
    new_momentum = nesterov * momentum + average
    new_outer = outer_weights - outer_rate * (average + nesterov * new_momentum)
    rounded = new_outer.astype(jnp.bfloat16)
    stacked = lax.all_gather(
        rounded.reshape(1, flat_rows, rounded.shape[1]), "rep", axis=0, tiled=True
    )
    spread = lax.all_to_all(stacked, "tp", split_axis=2, concat_axis=1, tiled=True)
    weights = spread.reshape(width, local_cols)
    return (weights, new_outer, new_momentum)


def solution(mesh):
    in_specs = (
        P("rep", "tp", None),
        P("rep", None, "tp"),
        P("rep", None, "tp"),
        P(("rep", "tp"), None),
        P(("rep", "tp"), None),
    )
    out_specs = (P(None, "tp"), P(("rep", "tp"), None), P(("rep", "tp"), None))
    return jax.shard_map(
        on_device, mesh=mesh, in_specs=in_specs, out_specs=out_specs, check_vma=False
    )
```

profile of v0, /device:TPU:0, one launch (start us, length us, event | category | flops | bytes accessed | tf_op | source)
XLA Modules:
  0.0 679.7 jit_solution(12934567029889370212)
XLA Ops:
  7.2 0.0 all-gather.4.cloned.1.call-start
  7.2 0.7 all-gather.4.cloned.1.call-update
  7.9 0.0 reduce-scatter.2.cloned.1.call-start
  7.9 232.2 %all-gather.4.cloned.1.call-done = bf16[1,2048,4096]{2,1,0:T(8,128)(2,1)} async-done(((bf16[1,256,4096]{2,1,0:T(8,128)(2,1)}), bf16[1,2048,4096]{2,1,0:T(8,128)(2,1)}) %all-gather.4.cloned.1.call-update) | async-done | bytes 16777232 | tf_op jit(solution)/shard_map/all_gather | solution.py:18
  240.1 25.8 %fusion = bf16[4096,1024]{1,0:T(8,128)(2,1)} fusion(bf16[1,4096,1024]{2,1,0:T(8,128)(2,1)} %param.7, bf16[1,2048,4096]{2,1,0:T(8,128)(2,1)} %all-gather.4.cloned.1.call-done, bf16[1,2048,1024]{2,1,0:T(8,128)(2,1)} %param.6), kind=kOutput, calls=%fused_computation.1 | convolution fusion | flops 17192452096 | bytes 37748736 | tf_op jit(solution)/shard_map/td,tf->df/dot_general | solution.py:16
  266.0 0.0 reduce-scatter.2.cloned.1.call-update
  266.0 0.0 all-gather.6.cloned.1.call-start
  266.0 69.7 %reduce-scatter.2.cloned.1.call-done = bf16[1024,1024]{1,0:T(8,128)(2,1)} async-done(((bf16[4096,1024]{1,0:T(8,128)(2,1)}), bf16[1024,1024]{1,0:T(8,128)(2,1)}) %reduce-scatter.2.cloned.1.call-update) | async-done | bytes 2097168 | tf_op jit(solution)/shard_map/reduce_scatter | solution.py:23
  335.7 53.6 %all_to_all.28 = bf16[8,128,1024]{2,1,0:T(8,128)(2,1)S(1)} all-to-all(bf16[8,128,1024]{2,1,0:T(8,128)(2,1)} %bitcast.25), channel_id=1, replica_groups=mesh['rep'=4,'tp'=8] {'tp'}, dimensions={0} | all-to-all | bytes 4194304 | tf_op jit(solution)/shard_map/all_to_all | solution.py:26
  389.3 0.6 multiply_bitcast_fusion
  389.9 0.0 copy-start
  389.9 0.3 copy.14
  390.2 1.9 copy-done
  392.1 7.9 %fusion.6 = (bf16[128,8192]{1,0:T(8,128)(2,1)}, f32[128,8192]{1,0:T(8,128)}, f32[128,8192]{1,0:T(8,128)}) fusion(f32[128,8192]{1,0:T(8,128)S(1)} %copy-done, f32[128,8192]{1,0:T(8,128)S(1)} %bitcast.22, f32[128,8192]{1,0:T(8,128)} %param.9), kind=kLoop, calls=%fused_computation.8 | loop fusion | flops 7340032 | bytes 23068672 | tf_op jit(solution)/shard_map/convert_element_type | solution.py:32
  399.9 0.0 all-gather.6.cloned.1.call-update
  400.0 56.5 %all-gather.6.cloned.1.call-done = bf16[512,8192]{1,0:T(8,128)(2,1)} async-done(((bf16[128,8192]{1,0:T(8,128)(2,1)}), bf16[512,8192]{1,0:T(8,128)(2,1)}) %all-gather.6.cloned.1.call-update) | async-done | bytes 8388624 | tf_op jit(solution)/shard_map/all_gather | solution.py:33
  456.5 13.6 %copy.13 = bf16[4,128,8192]{1,0,2:T(4,128)(2,1)} copy(bf16[4,128,8192]{2,1,0:T(8,128)(2,1)} %bitcast.24) | data formatting | bytes 16777216 | tf_op jit(solution)/shard_map/all_gather | solution.py:33
  470.1 189.4 %all_to_all.29 = bf16[4,128,8192]{1,0,2:T(4,128)(2,1)} all-to-all(bf16[4,128,8192]{1,0,2:T(4,128)(2,1)} %copy.13), channel_id=1, replica_groups=mesh['rep'=4,'tp'=8] {'tp'}, dimensions={2} | all-to-all | bytes 16777216 | tf_op jit(solution)/shard_map/all_to_all | solution.py:36
  659.5 13.6 %copy.12 = bf16[4,8,128,1024]{3,2,1,0:T(8,128)(2,1)} copy(bf16[4,8,128,1024]{2,0,3,1:T(4,128)(2,1)} %bitcast.21) | data formatting | bytes 16777216 | tf_op jit(solution)/shard_map/all_to_all | solution.py:36
Async XLA Ops:
  7.2 233.0 %all-gather.4.cloned.1.call-start = ((), (), s32[]{:S(2)}) async-start(), calls=%async_computation.3 | async-start | bytes 18874368 | tf_op jit(solution)/shard_map/all_gather | solution.py:18
  7.9 327.8 %reduce-scatter.2.cloned.1.call-start = ((), (), s32[]{:S(2)}) async-start(), calls=%async_computation.4 | async-start | bytes 10485760 | tf_op jit(solution)/shard_map/reduce_scatter | solution.py:23
  266.0 190.5 %all-gather.6.cloned.1.call-start = ((), (), s32[]{:S(2)}) async-start(), calls=%async_computation.5 | async-start | bytes 10485760 | tf_op jit(solution)/shard_map/all_gather | solution.py:33
  389.9 2.2 copy-start
Sparse Core Ops, SparseCore 0:
  10.1 229.9 all-gather.3
  266.1 69.5 reduce-scatter.1
  400.1 56.3 all-gather.5
where the time goes:
time: 681 us; the launch traced here: 680 us
  waiting for transfers between devices  359 us (53%)
  blocking collectives  243 us (36%)
  local copies, waits for them, and re-layouts  29.4 us (4%)
  matrix products  25.8 us (4%)
  between operations  13.8 us (2%)
  other arithmetic  8.45 us (1%)
    all_gather x1, waiting for transfers between devices, on_device(): lax.all_gather(activations, 'tp', axis=1, tiled=True)[0]  232 us
    all_to_all x1, blocking collectives, on_device(): lax.all_to_all(stacked, 'tp', split_axis=2, concat_axis=1, tiled=True)  189 us
    reduce_scatter x1, waiting for transfers between devices, on_device(): lax.psum_scatter(delta.astype(jnp.float32).astype(jnp.bfloat16), 'rep', s...  69.7 us
    all_gather x1, waiting for transfers between devices, on_device(): lax.all_gather(rounded.reshape(1, flat_rows, rounded.shape[1]), 'rep', ax...  56.5 us
    all_to_all x1, blocking collectives, on_device(): lax.all_to_all(summed.astype(jnp.bfloat16), 'tp', split_axis=0, concat_ax...  53.6 us
    dot_general x1, matrix products, on_device(): jnp.einsum('td,tf->df', lax.all_gather(activations, 'tp', axis=1, tiled=T...  25.8 us
  transfers between devices with their start and end apart: 3, of which 3 were waited for; matrix products, arithmetic and copies ran while one was open for 0% of the time, Pallas kernels for 0%

commit v1 on v0

--- a/solution.py
+++ b/solution.py
@@ -10,9 +10,6 @@
 def on_device(activations, cotangent, drift, outer_weights, momentum):
     replicas = lax.axis_size("rep")
     cot_rows = cotangent[0]
-    width = activations.shape[2]
-    local_cols = cot_rows.shape[1]
-    flat_rows = outer_weights.shape[0]
     grad = jnp.einsum(
         "td,tf->df",
         lax.all_gather(activations, "tp", axis=1, tiled=True)[0],
@@ -30,11 +27,8 @@
     new_momentum = nesterov * momentum + average
     new_outer = outer_weights - outer_rate * (average + nesterov * new_momentum)
     rounded = new_outer.astype(jnp.bfloat16)
-    stacked = lax.all_gather(
-        rounded.reshape(1, flat_rows, rounded.shape[1]), "rep", axis=0, tiled=True
-    )
-    spread = lax.all_to_all(stacked, "tp", split_axis=2, concat_axis=1, tiled=True)
-    weights = spread.reshape(width, local_cols)
+    spread = lax.all_to_all(rounded, "tp", split_axis=1, concat_axis=0, tiled=True)
+    weights = lax.all_gather(spread, "rep", axis=0, tiled=True)
     return (weights, new_outer, new_momentum)
 
 

time: 681 us -> 533 us (0.78)
  blocking collectives: 243 us -> 51.9 us
  waiting for transfers between devices: 359 us -> 384 us
  local copies, waits for them, and re-layouts: 29.4 us -> 38.6 us
    all_to_all x2 -> x1, blocking collectives: 243 us -> 51.9 us  [on_device(): lax.all_to_all(rounded, 'tp', split_axis=1, concat_axis=0, tiled=True)]
    all_to_all x0 -> x1, waiting for transfers between devices: none -> 36.7 us  [on_device(): lax.all_to_all(summed.astype(jnp.bfloat16), 'tp', split_axis=0, concat_ax...]
    unnamed x2 -> x5, local copies, waits for them, and re-layouts: 1.87 us -> 30.5 us
    all_gather x1 -> x0, local copies, waits for them, and re-layouts: 13.6 us -> none  [on_device(): lax.all_gather(rounded.reshape(1, flat_rows, rounded.shape[1]), 'rep', ax...]
    all_gather x1, waiting for transfers between devices: 56.5 us -> 45 us  [on_device(): weights = lax.all_gather(spread, 'rep', axis=0, tiled=True)]
    all_to_all x1, local copies, waits for them, and re-layouts: 13.6 us -> 2.85 us  [on_device(): lax.all_to_all(rounded, 'tp', split_axis=1, concat_axis=0, tiled=True)]
  transfers between devices with their start and end apart: 3 -> 4, of which waited for: 3 -> 4; matrix products, arithmetic and copies ran while one was open for 0% -> 4% of each run, Pallas kernels for 0% -> 0%
where the time goes in v1:
time: 533 us
  waiting for transfers between devices  384 us (72%)
  blocking collectives  51.9 us (10%)
  local copies, waits for them, and re-layouts  38.6 us (7%)
  matrix products  25.8 us (5%)
  between operations  13.8 us (3%)
  other arithmetic  12.3 us (2%)
  starting transfers between devices  5.8 us (1%)
    all_gather x1, waiting for transfers between devices, on_device(): lax.all_gather(activations, 'tp', axis=1, tiled=True)[0]  232 us
    reduce_scatter x1, waiting for transfers between devices, on_device(): lax.psum_scatter(delta.astype(jnp.float32).astype(jnp.bfloat16), 'rep', s...  69.8 us
    all_to_all x1, blocking collectives, on_device(): lax.all_to_all(rounded, 'tp', split_axis=1, concat_axis=0, tiled=True)  51.9 us
    all_gather x1, waiting for transfers between devices, on_device(): weights = lax.all_gather(spread, 'rep', axis=0, tiled=True)  45 us
    all_to_all x1, waiting for transfers between devices, on_device(): lax.all_to_all(summed.astype(jnp.bfloat16), 'tp', split_axis=0, concat_ax...  36.7 us
    unnamed x5, local copies, waits for them, and re-layouts  30.5 us
    dot_general x1, matrix products, on_device(): jnp.einsum('td,tf->df', lax.all_gather(activations, 'tp', axis=1, tiled=T...  25.8 us
  transfers between devices with their start and end apart: 4, of which 4 were waited for; matrix products, arithmetic and copies ran while one was open for 4% of the time, Pallas kernels for 0%

profile of v1, /device:TPU:0, one launch (start us, length us, event | category | flops | bytes accessed | tf_op | source)
XLA Modules:
  0.0 532.6 jit_solution(2489531201938662445)
XLA Ops:
  7.2 0.0 all-gather.3.cloned.1.call-start
  7.2 0.7 all-gather.3.cloned.1.call-update
  7.9 0.0 reduce-scatter.2.cloned.1.call-start
  7.9 232.2 %all-gather.3.cloned.1.call-done = bf16[1,2048,4096]{2,1,0:T(8,128)(2,1)} async-done(((bf16[1,256,4096]{2,1,0:T(8,128)(2,1)}), bf16[1,2048,4096]{2,1,0:T(8,128)(2,1)}) %all-gather.3.cloned.1.call-update) | async-done | bytes 16777232 | tf_op jit(solution)/shard_map/all_gather | solution.py:15
  240.1 25.8 %fusion = bf16[4096,1024]{1,0:T(8,128)(2,1)} fusion(bf16[1,4096,1024]{2,1,0:T(8,128)(2,1)} %param.7, bf16[1,2048,4096]{2,1,0:T(8,128)(2,1)} %all-gather.3.cloned.1.call-done, bf16[1,2048,1024]{2,1,0:T(8,128)(2,1)} %param.6), kind=kOutput, calls=%fused_computation.1 | convolution fusion | flops 17192452096 | bytes 37748736 | tf_op jit(solution)/shard_map/td,tf->df/dot_general | solution.py:13
  266.0 0.0 reduce-scatter.2.cloned.1.call-update
  266.0 69.8 %reduce-scatter.2.cloned.1.call-done = bf16[1024,1024]{1,0:T(8,128)(2,1)} async-done(((bf16[4096,1024]{1,0:T(8,128)(2,1)}), bf16[1024,1024]{1,0:T(8,128)(2,1)}) %reduce-scatter.2.cloned.1.call-update) | async-done | bytes 2097168 | tf_op jit(solution)/shard_map/reduce_scatter | solution.py:20
  335.7 5.5 %all-to-all-start = ((bf16[8,128,1024]{2,1,0:T(8,128)(2,1)}), bf16[8,128,1024]{2,1,0:T(8,128)(2,1)S(1)}, u32[]{:S(2)}, u32[]{:S(2)}) async-start(bf16[8,128,1024]{2,1,0:T(8,128)(2,1)} %bitcast.30), calls=%async_computation.1 | async-start | bytes 4194304 | tf_op jit(solution)/shard_map/all_to_all | solution.py:23
  341.2 0.2 all-gather.5.cloned.1.call-start
  341.5 5.6 %copy.13 = f32[128,8192]{0,1:T(8,128)} copy(f32[128,8192]{1,0:T(8,128)} %param.8) | data formatting | bytes 8388608 | tf_op args[3]
  347.0 5.6 %copy.12 = f32[128,8192]{0,1:T(8,128)} copy(f32[128,8192]{1,0:T(8,128)} %param.9) | data formatting | bytes 8388608 | tf_op args[4]
  352.6 36.7 %all-to-all-done = bf16[8,128,1024]{2,1,0:T(8,128)(2,1)S(1)} async-done(((bf16[8,128,1024]{2,1,0:T(8,128)(2,1)}), bf16[8,128,1024]{2,1,0:T(8,128)(2,1)S(1)}, u32[]{:S(2)}, u32[]{:S(2)}) %all-to-all-start) | async-done | bytes 2097184 | tf_op jit(solution)/shard_map/all_to_all | solution.py:23
  389.3 2.6 multiply_bitcast_fusion
  391.9 5.3 %copy.11 = f32[128,8,1024]{0,2,1:T(8,128)} copy(f32[128,8,1024]{2,0,1:T(8,128)} %multiply_bitcast_fusion) | data formatting | bytes 8388608 | tf_op jit(solution)/shard_map/div | solution.py:26
  397.3 9.7 %fusion.8 = (bf16[128,8192]{0,1:T(8,128)(2,1)}, f32[128,8192]{0,1:T(8,128)}, f32[128,8192]{0,1:T(8,128)}) fusion(f32[128,8192]{0,1:T(8,128)} %copy.13, f32[128,8192]{0,1:T(8,128)} %copy.12, f32[128,8,1024]{0,2,1:T(8,128)} %copy.11), kind=kLoop, calls=%fused_computation.10 | loop fusion | flops 7340032 | bytes 23068672 | tf_op jit(solution)/shard_map/convert_element_type | solution.py:29
  406.9 2.9 copy.14
  409.8 51.9 %all_to_all.32 = bf16[128,8,1024]{2,0,1:T(8,128)(2,1)} all-to-all(bf16[128,8,1024]{2,0,1:T(8,128)(2,1)S(1)} %copy.14), channel_id=1, replica_groups=mesh['rep'=4,'tp'=8] {'tp'}, dimensions={1} | all-to-all | bytes 4194304 | tf_op jit(solution)/shard_map/all_to_all | solution.py:30
  461.7 0.0 all-gather.5.cloned.1.call-update
  461.7 5.6 %copy.15 = f32[128,8192]{1,0:T(8,128)} copy(f32[128,8192]{0,1:T(8,128)} %get-tuple-element.7) | data formatting | bytes 8388608
  467.4 6.0 %copy.16 = f32[128,8192]{1,0:T(8,128)} copy(f32[128,8192]{0,1:T(8,128)} %get-tuple-element.8) | data formatting | bytes 8388608
  473.3 45.0 %all-gather.5.cloned.1.call-done = bf16[4096,1024]{1,0:T(8,128)(2,1)} async-done(((bf16[1024,1024]{1,0:T(8,128)(2,1)}), bf16[4096,1024]{1,0:T(8,128)(2,1)}) %all-gather.5.cloned.1.call-update) | async-done | bytes 8388624 | tf_op jit(solution)/shard_map/all_gather | solution.py:31
  518.3 7.8 %copy.18 = bf16[4096,1024]{1,0:T(8,128)(2,1)} copy(bf16[4096,1024]{1,0:T(8,128)(2,1)} %all-gather.5.cloned.1.call-done) | data formatting | bytes 16777216
Async XLA Ops:
  7.2 233.0 %all-gather.3.cloned.1.call-start = ((), (), s32[]{:S(2)}) async-start(), calls=%async_computation.3 | async-start | bytes 18874368 | tf_op jit(solution)/shard_map/all_gather | solution.py:15
  7.9 327.8 %reduce-scatter.2.cloned.1.call-start = ((), (), s32[]{:S(2)}) async-start(), calls=%async_computation.4 | async-start | bytes 10485760 | tf_op jit(solution)/shard_map/reduce_scatter | solution.py:20
  335.7 53.6 %all-to-all-start = ((bf16[8,128,1024]{2,1,0:T(8,128)(2,1)}), bf16[8,128,1024]{2,1,0:T(8,128)(2,1)S(1)}, u32[]{:S(2)}, u32[]{:S(2)}) async-start(bf16[8,128,1024]{2,1,0:T(8,128)(2,1)} %bitcast.30), calls=%async_computation.1 | async-start | bytes 4194304 | tf_op jit(solution)/shard_map/all_to_all | solution.py:23
  341.2 177.0 %all-gather.5.cloned.1.call-start = ((), (), s32[]{:S(2)}) async-start(), calls=%async_computation.5 | async-start | bytes 10485760 | tf_op jit(solution)/shard_map/all_gather | solution.py:31
Sparse Core Ops, SparseCore 0:
  10.1 229.9 all-gather.2
  266.1 69.5 reduce-scatter.1
  461.9 56.3 all-gather.4

commit v2 on v1

v2 whole, which is shorter than its diff:
```python
import functools
import math

import jax
import jax.numpy as jnp
from jax import lax
from jax.experimental import pallas as pl
from jax.experimental.pallas import tpu as pltpu
from jax.sharding import PartitionSpec as P


outer_rate = 0.7
nesterov = 0.9


def cut(rows):
    if rows % 128:
        return ((0, rows),)
    unit = rows // 4
    return ((2 * unit, unit), (0, 2 * unit), (3 * unit, unit))


f32, bf16 = jnp.float32, jnp.bfloat16


def sort_kernel(inner, outer, rows, strips, at_ref, acts_ref, *refs):
    out_refs, masks = refs[: inner * len(strips)], refs[inner * len(strips) :]
    span = acts_ref.shape[1]

    if not masks:
        to = lax.broadcasted_iota(jnp.int32, (rows, rows), 0)
        same = jnp.where(to == lax.broadcasted_iota(jnp.int32, (rows, rows), 1), 1.0, 0.0).astype(bf16)
        for k in range(inner):
            for i in range(outer):
                start = pl.multiple_of((i * inner + lax.rem(at_ref[0] + k, inner)) * rows, rows)
                turned = lax.dot_general(
                    same, acts_ref[:, pl.ds(start, rows)], (((1,), (1,)), ((), ())), preferred_element_type=f32
                ).astype(bf16)
                for q, (low, strip) in enumerate(strips):
                    out_refs[k * len(strips) + q][i * strip : (i + 1) * strip] = turned[low : low + strip]
        return

    @pl.when(pl.program_id(0) == 0)
    def _():
        for q, (low, strip) in enumerate(strips):
            m = outer * strip
            to = lax.broadcasted_iota(jnp.int32, (m, span), 0)
            source = lax.broadcasted_iota(jnp.int32, (m, span), 1)
            base = lax.shift_right_logical(to, strip.bit_length() - 1) * (inner * rows) + (to & (strip - 1)) + low
            for k in range(inner):
                column = lax.rem(at_ref[0] + k, inner) * rows
                masks[k * len(strips) + q][...] = jnp.where(source == base + column, 1.0, 0.0).astype(bf16)

    for mask, out_ref in zip(masks, out_refs):
        out_ref[...] = lax.dot_general(
            mask[...], acts_ref[...], (((1,), (1,)), ((), ())), preferred_element_type=f32
        ).astype(bf16)


def sort_columns(acts, at, inner, outer, rows, strips):
    tokens, width = acts.shape
    reps = at.shape[0] - 1
    span = width // reps
    return pl.pallas_call(
        functools.partial(sort_kernel, inner, outer, rows, strips),
        grid_spec=pltpu.PrefetchScalarGridSpec(
            num_scalar_prefetch=1,
            grid=(reps,),
            in_specs=[pl.BlockSpec((tokens, span), lambda j, at: (0, at[1 + j]))],
            out_specs=[pl.BlockSpec((outer * size, tokens), lambda j, at: (j, 0)) for _ in range(inner) for _, size in strips],
            scratch_shapes=[pltpu.VMEM((outer * size, span), bf16) for _ in range(inner) for _, size in strips if rows % 128],
        ),
        out_shape=[jax.ShapeDtypeStruct((reps * outer * size, tokens), bf16) for _ in range(inner) for _, size in strips],
        cost_estimate=pl.CostEstimate(flops=2 * tokens * width * span, bytes_accessed=4 * tokens * width, transcendentals=0),
    )(at, acts)


def dot_kernel(outer, inner, count, at_ref, *refs):
    blocks, cots = refs[: outer * inner], refs[outer * inner : outer * inner + count]
    away_ref, here_ref = refs[-2:]
    depth = blocks[0].shape[1]
    half = away_ref.shape[0]
    for i in range(count):

        @pl.when(pl.program_id(0) == i)
        def _(i=i):
            total = None
            for s in range(outer):
                for k in range(inner):
                    owner = lax.rem(at_ref[1] + (outer - s), outer) * inner + lax.rem(at_ref[0] + (inner - k), inner)
                    start = pl.multiple_of(owner * depth, depth)
                    term = jnp.dot(blocks[s * inner + k][...], cots[i][pl.ds(start, depth), :], preferred_element_type=f32)
                    total = term if total is None else total + term
            here_ref[...] = total[:half]
            away_ref[...] = total[half:].astype(away_ref.dtype)


def partial_grad(blocks, cots, at, outer, first=0, held=()):
    count = len(cots)
    inner = len(blocks) // outer
    m, depth = blocks[0].shape
    tokens, cols = cots[0].shape
    tile = min(cols, 512)
    tiles = cols // tile

    def cot_spec(k):
        return pl.BlockSpec((tokens, tile), lambda i, j, at: (0, jnp.where(i == k, j, jnp.where(i < k, 0, tiles - 1))))

    out = pl.BlockSpec((m // 2, tile), lambda i, j, at: (0, lax.rem(at[0] + (2 * inner - first - i), inner) * tiles + j))
    return pl.pallas_call(
        functools.partial(dot_kernel, outer, inner, count),
        grid_spec=pltpu.PrefetchScalarGridSpec(
            num_scalar_prefetch=1,
            grid=(count, tiles),
            in_specs=[pl.BlockSpec((m, depth), lambda i, j, at: (0, 0)) for _ in blocks]
            + [cot_spec(k) for k in range(count)]
            + [pl.BlockSpec(memory_space=pl.ANY) for _ in held],
            out_specs=[out, out],
        ),
        out_shape=[jax.ShapeDtypeStruct((m // 2, inner * cols), d) for d in (bf16, f32)],
        input_output_aliases={1 + len(blocks) + count + i: i for i in range(len(held))},
        cost_estimate=pl.CostEstimate(
            flops=2 * m * tokens * count * cols, bytes_accessed=2 * (m * tokens + tokens * count * cols + 2 * m * count * cols), transcendentals=0
        ),
    )(at, *blocks, *cots, *held)


def step_kernel(outer, reps, at_ref, *refs):
    parts, (weights_ref, momentum_ref) = refs[:outer], refs[outer : outer + 2]
    new_weights_ref, new_momentum_ref, *rounded = refs[-2 - outer :]
    for k in range(outer):

        @pl.when(pl.program_id(0) == k)
        def _(k=k):
            average = parts[k][...].astype(f32) / reps
            new_momentum = nesterov * momentum_ref[...] + average
            new_weights = weights_ref[...] - outer_rate * (average + nesterov * new_momentum)
            new_momentum_ref[...] = new_momentum
            new_weights_ref[...] = new_weights
            rounded[k][...] = new_weights.astype(bf16)


def outer_step(parts, weights, momentum, held, at, low, reps):
    outer = len(parts)
    strip, span = parts[0].shape
    small = pl.BlockSpec((strip, span), lambda k, at: (0, 0))
    state = pl.BlockSpec((strip, span), lambda k, at: (low // strip, lax.rem(at[1] + (outer - k), outer)))
    shape = jax.ShapeDtypeStruct(weights.shape, f32)
    out = pl.pallas_call(
        functools.partial(step_kernel, outer, reps),
        grid_spec=pltpu.PrefetchScalarGridSpec(
            num_scalar_prefetch=1,
            grid=(outer,),
            in_specs=[small] * outer + [state, state] + [pl.BlockSpec(memory_space=pl.ANY)] * len(held),
            out_specs=[state, state] + [small] * outer,
        ),
        out_shape=[shape, shape] + [jax.ShapeDtypeStruct((strip, span), bf16)] * outer,
        input_output_aliases={outer + 3 + i: i for i in range(len(held))},
        cost_estimate=pl.CostEstimate(flops=8 * outer * strip * span, bytes_accessed=20 * outer * strip * span, transcendentals=0),
    )(at, *parts, weights, momentum, *held)
    return out[:2], out[2:]


def spread_kernel(outer, inner, at_ref, *refs):
    ins, outs = refs[: outer * inner], refs[outer * inner :]
    for k in range(outer):
        index = lax.rem(at_ref[1] + (outer - k), outer)
        for j in range(inner):
            outs[j][index] = ins[k * inner + j][...]


def spread(parts, at, inner):
    outer = len(parts)
    strip, span = parts[0].shape
    cols = span // inner

    def column(j):
        return pl.BlockSpec((strip, cols), lambda i, at: (0, lax.rem(at[0] + j, inner)))

    return pl.pallas_call(
        functools.partial(spread_kernel, outer, inner),
        grid_spec=pltpu.PrefetchScalarGridSpec(
            num_scalar_prefetch=1,
            grid=(1,),
            in_specs=[column(j) for _ in range(outer) for j in range(inner)],
            out_specs=[pl.BlockSpec((outer, strip, cols), lambda i, at: (0, 0, 0))] * inner,
        ),
        out_shape=[jax.ShapeDtypeStruct((outer, strip, cols), bf16)] * inner,
        cost_estimate=pl.CostEstimate(flops=0, bytes_accessed=4 * outer * strip * span, transcendentals=0),
    )(at, *[p for p in parts for _ in range(inner)])


def write_kernel(count, low, at_ref, *refs):
    out_ref, sems = refs[-2:]
    strip = refs[0].shape[1]
    copies = []
    for i in range(count):
        target = out_ref.at[at_ref[3 * i], at_ref[3 * i + 1], :, at_ref[3 * i + 2], pl.ds(low, strip), :]
        copies.append(pltpu.make_async_copy(refs[i], target, sems.at[i]))
        copies[-1].start()
    for copy in copies:
        copy.wait()


def write(found, at, held, shape, low):
    small = pl.BlockSpec(found[0].shape, lambda i, at: (0, 0, 0))
    more = [] if held is None else [held]
    return pl.pallas_call(
        functools.partial(write_kernel, len(found), low),
        grid_spec=pltpu.PrefetchScalarGridSpec(
            num_scalar_prefetch=1,
            grid=(1,),
            in_specs=[small] * len(found) + [pl.BlockSpec(memory_space=pl.ANY) for _ in more],
            out_specs=pl.BlockSpec(memory_space=pltpu.HBM),
            scratch_shapes=[pltpu.SemaphoreType.DMA((len(found),))],
        ),
        out_shape=jax.ShapeDtypeStruct(shape, bf16),
        input_output_aliases={1 + len(found) + i: i for i in range(len(more))},
        cost_estimate=pl.CostEstimate(flops=0, bytes_accessed=4 * len(found) * found[0].size, transcendentals=0),
    )(at, *found, *more)


def add_kernel(high, here_ref, away_ref, *out_refs):
    for j in range(1, high):

        @pl.when(pl.program_id(0) == j - 1)
        def _(j=j):
            out_refs[j - 1][...] = (here_ref[...] + away_ref[...].astype(f32)).astype(bf16)


def chip_sum(here, away, high):
    m, width = here.shape
    block = pl.BlockSpec((m // high, width // 2), lambda j, i: (j + 1, i))
    return pl.pallas_call(
        functools.partial(add_kernel, high),
        grid=(high - 1, 2),
        in_specs=[block, block],
        out_specs=[
            pl.BlockSpec((m // high, width // 2), lambda j, i, k=k: (0, jnp.where(j == k, i, jnp.where(j < k, 0, 1)))) for k in range(high - 1)
        ],
        out_shape=[jax.ShapeDtypeStruct((m // high, width), bf16) for _ in range(high - 1)],
        cost_estimate=pl.CostEstimate(flops=m * width, bytes_accessed=8 * m * width * (high - 1) // high, transcendentals=0),
    )(here, away)


def total_kernel(outer, inner, strip, at_ref, here_ref, away_ref, *refs):
    outs = refs[-outer:]
    drifts = refs[-outer - inner : -outer]
    got = refs[: -outer - inner]
    cols = here_ref.shape[1] // inner
    for k in range(outer):
        index = lax.rem(at_ref[1] + k, outer)
        at_rows = pl.ds(pl.multiple_of(index * strip, strip), strip)
        for j in range(inner):
            at_cols = pl.ds(pl.multiple_of(lax.rem(at_ref[0] + (inner - j), inner) * cols, cols), cols)
            total = here_ref[at_rows, at_cols] + away_ref[at_rows, at_cols].astype(f32) + drifts[j][index].astype(f32)
            for ref in got:
                total = total + ref[at_rows, at_cols].astype(f32)
            outs[k][:, at_cols] = total.astype(bf16)


def full_sum(here, away, got, drifts, at, outer, low, strip):
    inner = len(drifts)
    cols = drifts[0].shape[2]
    span = inner * cols
    rows = pl.BlockSpec((outer * strip, span), lambda i, at: (0, 0))
    return pl.pallas_call(
        functools.partial(total_kernel, outer, inner, strip),
        grid_spec=pltpu.PrefetchScalarGridSpec(
            num_scalar_prefetch=1,
            grid=(1,),
            in_specs=[rows] * (2 + len(got)) + [pl.BlockSpec((outer, strip, cols), lambda i, at: (0, low // strip, 0)) for _ in drifts],
            out_specs=[pl.BlockSpec((strip, span), lambda i, at: (0, 0))] * outer,
        ),
        out_shape=[jax.ShapeDtypeStruct((strip, span), bf16)] * outer,
        cost_estimate=pl.CostEstimate(flops=4 * outer * strip * span, bytes_accessed=12 * outer * strip * span, transcendentals=0),
    )(at, here, away, *got, *drifts)


def take_kernel(at_ref, in_ref, out_ref):
    out_ref[...] = in_ref[...]


def take(array, at, count):
    _, rows, cols = array.shape
    return pl.pallas_call(
        take_kernel,
        grid_spec=pltpu.PrefetchScalarGridSpec(
            num_scalar_prefetch=1,
            grid=(count, 2),
            in_specs=[pl.BlockSpec((1, rows // 2, cols), lambda j, i, at: (at[j], i, 0))],
            out_specs=pl.BlockSpec((1, rows // 2, cols), lambda j, i, at: (j, i, 0)),
        ),
        out_shape=jax.ShapeDtypeStruct((count, rows, cols), array.dtype),
        cost_estimate=pl.CostEstimate(flops=0, bytes_accessed=4 * count * rows * cols, transcendentals=0),
    )(at, array)


def twin_kernel(count, at_ref, mine_ref, got_ref, *out_refs):
    for j in range(count):

        @pl.when(pl.program_id(0) == j)
        def _(j=j):
            out_refs[j][...] = (mine_ref[0].astype(f32) + got_ref[0].astype(f32)).astype(bf16)


def twin_sum(mine, got, at):
    count, rows, cols = got.shape
    count -= 1
    return pl.pallas_call(
        functools.partial(twin_kernel, count),
        grid_spec=pltpu.PrefetchScalarGridSpec(
            num_scalar_prefetch=1,
            grid=(count, 2),
            in_specs=[
                pl.BlockSpec((1, rows // 2, cols), lambda j, i, at: (at[j + 1], i, 0)),
                pl.BlockSpec((1, rows // 2, cols), lambda j, i, at: (j + 1, i, 0)),
            ],
            out_specs=[
                pl.BlockSpec((rows // 2, cols), lambda j, i, at, k=k: (jnp.where(j == k, i, jnp.where(j < k, 0, 1)), 0)) for k in range(count)
            ],
        ),
        out_shape=[jax.ShapeDtypeStruct((rows, cols), bf16) for _ in range(count)],
        cost_estimate=pl.CostEstimate(flops=count * rows * cols, bytes_accessed=6 * count * rows * cols, transcendentals=0),
    )(at, mine, got)


def drift_kernel(inner, at_ref, *refs):
    outs, ins = refs[-inner:], refs[:-inner]
    total = ins[0][0].astype(f32) + ins[1][0].astype(f32)
    for ref in ins[2:]:
        total = total + ref[...].astype(f32)
    for j in range(inner):

        @pl.when(pl.program_id(0) == j)
        def _(j=j):
            outs[j][0] = total.astype(bf16)


def drift_sum(mine, got, more, at, place, inner, outer):
    _, length, cols = mine.shape
    rows = length // (inner * outer)

    def part(j, i, ref):
        return i * inner + lax.rem(ref[0] + j, inner)

    return pl.pallas_call(
        functools.partial(drift_kernel, inner),
        grid_spec=pltpu.PrefetchScalarGridSpec(
            num_scalar_prefetch=1,
            grid=(inner, outer),
            in_specs=[
                pl.BlockSpec((1, rows, cols), lambda j, i, ref: (ref[2], part(j, i, ref), 0)),
                pl.BlockSpec((1, rows, cols), lambda j, i, ref: (0, part(j, i, ref), 0)),
            ]
            + [pl.BlockSpec((rows, cols), lambda j, i, ref: (part(j, i, ref), 0)) for _ in more],
            out_specs=[
                pl.BlockSpec((1, rows, cols), lambda j, i, ref, k=k: (jnp.where(j == k, i, jnp.where(j < k, 0, outer - 1)), 0, 0))
                for k in range(inner)
            ],
        ),
        out_shape=[jax.ShapeDtypeStruct((outer, rows, cols), bf16) for _ in range(inner)],
        cost_estimate=pl.CostEstimate(flops=3 * length * cols, bytes_accessed=8 * length * cols, transcendentals=0),
    )(jnp.concatenate([place, at[:1]]), mine, got, *more)


def on_device(activations, cotangent, drift, outer_weights, momentum):
    reps, tps = lax.axis_size("rep"), lax.axis_size("tp")
    inner = 2 ** (int(math.log2(tps)) // 2)
    outer = tps // inner
    pair = 2
    high = reps // pair
    rep, tp = lax.axis_index("rep"), lax.axis_index("tp")
    z, x = lax.div(tp, inner), lax.rem(tp, inner)
    y, c = lax.div(rep, pair), lax.rem(rep, pair)

    def over_x(v, k):
        return lax.ppermute(v, "tp", [(a * inner + b, a * inner + (b + k) % inner) for a in range(outer) for b in range(inner)])

    def over_z(v, k):
        return lax.ppermute(v, "tp", [(a * inner + b, (a + k) % outer * inner + b) for a in range(outer) for b in range(inner)])

    def over_y(v, k):
        return lax.ppermute(v, "rep", [(a * pair + b, (a + k) % high * pair + b) for a in range(high) for b in range(pair)])

    def over_c(v):
        return lax.ppermute(v, "rep", [(a, a ^ 1) for a in range(reps)])

    def ahead(index, k, n):
        return lax.rem(index + k, n)

    acts, cot = activations[0], cotangent[0]
    _, width = acts.shape
    cols = cot.shape[1]
    rows = outer_weights.shape[0]
    strips = cut(rows)
    n = len(strips)

    order = [ahead(y, jy, high) * pair + (c ^ jc) for jc in range(pair) for jy in range(high)]
    at = jnp.stack([x, *order]).astype(jnp.int32)
    place = jnp.stack([x, z]).astype(jnp.int32)
    own = sort_columns(acts, at, inner, outer, rows, strips)
    ring = [[own[q]] for q in range(n)]
    for q in range(n):
        for k in range(1, inner):
            ring[q].append(over_x(own[k * n + q], k))
    cots = [cot]
    for k in range(1, inner):
        cots.append(over_x(cot, k))
    for _ in range(1, outer):
        for q in range(n):
            for _ in range(inner):
                ring[q].append(over_z(ring[q][-inner], 1))

    mine = drift[0].reshape(reps, tps * rows, cols)
    near = jnp.stack(order[:high]).astype(jnp.int32)
    got = take(mine, near ^ 1, high)
    got = over_c(got)
    more = list(twin_sum(mine, got, near))
    for k in range(1, high):
        more[k - 1] = over_y(more[k - 1], k)
    drifts = list(drift_sum(mine, got, more, near, place, inner, outer))
    for k in range(1, inner):
        drifts[k] = over_x(drifts[k], k)

    weights, held = None, ()
    for q, (low, strip) in enumerate(strips):
        if q == 0:
            early = partial_grad(ring[q], cots[:1], place, outer)
            away, here = partial_grad(ring[q], cots[1:], place, outer, 1, early)
        else:
            away, here = partial_grad(ring[q], cots, place, outer)
        away = over_c(away)
        sent = chip_sum(here, away, high)
        got = []
        for j in range(1, high):
            got.append(over_y(sent[j - 1], j))
        parts = list(full_sum(here, away, got, drifts, place, outer, low, strip))
        for k in range(1, outer):
            parts[k] = over_z(parts[k], k)
        held, parts = outer_step(parts, outer_weights, momentum, held, place, low, reps)
        parts = list(parts)
        for k in range(1, outer):
            parts[k] = over_z(parts[k], outer - k)
        parts = list(spread(parts[:1] + parts[:0:-1], place, inner))
        for k in range(1, inner):
            parts[k] = over_x(parts[k], k)
        found, target = [], []
        for j in range(high):
            for k in range(inner):
                near = parts[k]
                if j > 0:
                    near = over_y(near, j)
                far = over_c(near)
                found += [near, far]
                for there in (c, c ^ 1):
                    target += [ahead(y, high - j, high), there, ahead(x, inner - k, inner)]
        weights = write(found, jnp.stack(target).astype(jnp.int32), weights, (high, pair, outer, inner, rows, cols), low)
    return (weights.reshape(width, cols), *held)


def solution(mesh):
    in_specs = (
        P("rep", "tp", None),
        P("rep", None, "tp"),
        P("rep", None, "tp"),
        P(("rep", "tp"), None),
        P(("rep", "tp"), None),
    )
    out_specs = (P(None, "tp"), P(("rep", "tp"), None), P(("rep", "tp"), None))

    return jax.shard_map(on_device, mesh=mesh, in_specs=in_specs, out_specs=out_specs, check_vma=False)
```

time: 533 us -> 479 us (0.90)
  Pallas kernels: 0 us -> 114 us
  waiting for transfers between devices: 384 us -> 286 us
  starting transfers between devices: 5.8 us -> 64.8 us
  blocking collectives: 51.9 us -> 0 us
  local copies, waits for them, and re-layouts: 38.6 us -> 9.8 us
  matrix products: 25.8 us -> 0 us
  between operations: 13.8 us -> 1.31 us
  other arithmetic: 12.3 us -> 1.91 us
    ppermute x0 -> x70, waiting for transfers between devices: none -> 286 us  [the longest x36 120 us: over_z(): lax.ppermute(v, 'tp', [(a * inner + b, (a + k) % outer * inner + b) for a...]
    all_gather x2 -> x0, waiting for transfers between devices: 277 us -> none  [the longest x1 232 us: on_device(): lax.all_gather(activations, 'tp', axis=1, tiled=True)[0]]
    pallas_call x0 -> x23, Pallas kernels: none -> 114 us  [the longest x4 37.6 us: partial_grad(): pl.pallas_call(functools.partial(dot_kernel, outer, inner, count), grid_s...]
    reduce_scatter x1 -> x0, waiting for transfers between devices: 69.8 us -> none  [on_device(): lax.psum_scatter(delta.astype(jnp.float32).astype(jnp.bfloat16), 'rep', s...]
    ppermute x0 -> x70, starting transfers between devices: none -> 64.8 us  [the longest x36 41.9 us: over_z(): lax.ppermute(v, 'tp', [(a * inner + b, (a + k) % outer * inner + b) for a...]
    all_to_all x1 -> x0, blocking collectives: 51.9 us -> none  [on_device(): lax.all_to_all(rounded, 'tp', split_axis=1, concat_axis=0, tiled=True)]
    all_to_all x1 -> x0, waiting for transfers between devices: 36.7 us -> none  [on_device(): lax.all_to_all(summed.astype(jnp.bfloat16), 'tp', split_axis=0, concat_ax...]
    dot_general x1 -> x0, matrix products: 25.8 us -> none  [on_device(): jnp.einsum('td,tf->df', lax.all_gather(activations, 'tp', axis=1, tiled=T...]
  transfers between devices with their start and end apart: 4 -> 70, of which waited for: 4 -> 22; matrix products, arithmetic and copies ran while one was open for 4% -> 1% of each run, Pallas kernels for 0% -> 22%
where the time goes in v2:
time: 479 us; the launch traced here: 478 us
  waiting for transfers between devices  286 us (60%)
  Pallas kernels  114 us (24%)
  starting transfers between devices  64.8 us (14%)
  local copies, waits for them, and re-layouts  9.8 us (2%)
    ppermute x36, waiting for transfers between devices, over_z(): lax.ppermute(v, 'tp', [(a * inner + b, (a + k) % outer * inner + b) for a...  120 us
    ppermute x8, waiting for transfers between devices, over_x(): lax.ppermute(v, 'tp', [(a * inner + b, a * inner + (b + k) % inner) for a...  104 us
    ppermute x10, waiting for transfers between devices, over_y(): lax.ppermute(v, 'rep', [(a * pair + b, (a + k) % high * pair + b) for a i...  59.7 us
    ppermute x36, starting transfers between devices, over_z(): lax.ppermute(v, 'tp', [(a * inner + b, (a + k) % outer * inner + b) for a...  41.9 us
    pallas_call x4, Pallas kernels, partial_grad(): pl.pallas_call(functools.partial(dot_kernel, outer, inner, count), grid_s...  37.6 us
    pallas_call x3, Pallas kernels, outer_step(): pl.pallas_call(functools.partial(step_kernel, outer, reps), grid_spec=plt...  16.4 us
    pallas_call x3, Pallas kernels, write(): pl.pallas_call(functools.partial(write_kernel, len(found), low), grid_spe...  12 us
    ppermute x10, starting transfers between devices, over_y(): lax.ppermute(v, 'rep', [(a * pair + b, (a + k) % high * pair + b) for a i...  11.9 us
  transfers between devices with their start and end apart: 70, of which 22 were waited for; matrix products, arithmetic and copies ran while one was open for 1% of the time, Pallas kernels for 22%

profile of v2, /device:TPU:0, one launch (start us, length us, event | category | flops | bytes accessed | tf_op | source)
XLA Modules:
  0.0 478.0 jit_solution(5517146437518693431)
XLA Ops:
  1.3 5.4 %shard_map.79 = bf16[2,1024,1024]{2,1,0:T(8,128)(2,1)} custom-call(s32[2]{0:T(128)} %get-tuple-element.107.at_ref, bf16[4,1024,1024]{2,1,0:T(8,128)(2,1)} %bitcast.16), custom_call_target="tpu_custom_call" | custom-call | bytes 8388608 | tf_op jit(solution)/shard_map/pallas_call | solution.py:286
  7.2 2.5 collective-permute-start.7
  10.3 4.8 %shard_map.76 = (bf16[512,256]{1,0:T(8,128)(2,1)}, bf16[1024,256]{1,0:T(8,128)(2,1)}, bf16[512,256]{1,0:T(8,128)(2,1)}, bf16[512,256]{1,0:T(8,128)(2,1)}, bf16[1...) custom-call(s32[5]{0:T(128)} %stack.46.at_ref, bf16[256,4096]{1,0:T(8,128)(2,1)} %bitcast.24), custom_call_target="tpu_custom_call" | custom-call | flops 2147483648 | bytes 4194304 | tf_op jit(solution)/shard_map/pallas_call | solution.py:64
  17.3 95.1 %collective-permute-done.16.refs_1_ = bf16[1024,256]{1,0:T(8,128)(2,1)S(1)} collective-permute-done((bf16[1024,256]{1,0:T(8,128)(2,1)}, bf16[1024,256]{1,0:T(8,128)(2,1)S(1)}, u32[]{:S(2)}, u32[]{:S(2)}) %collective-permute-start.16) | collective-permute-done | bytes 524320 | tf_op jit(solution)/shard_map/ppermute | solution.py:378
  115.8 13.2 %collective-permute-done.18.refs_3_ = bf16[1024,256]{1,0:T(8,128)(2,1)S(1)} collective-permute-done((bf16[1024,256]{1,0:T(8,128)(2,1)S(1)}, bf16[1024,256]{1,0:T(8,128)(2,1)S(1)}, u32[]{:S(2)}, u32[]{:S(2)}) %collective-permute-start.18) | collective-permute-done | bytes 524320 | tf_op jit(solution)/shard_map/ppermute | solution.py:381
  129.0 11.2 %collective-permute-done.19.refs_4_ = bf16[1024,256]{1,0:T(8,128)(2,1)S(1)} collective-permute-done((bf16[1024,256]{1,0:T(8,128)(2,1)S(1)}, bf16[1024,256]{1,0:T(8,128)(2,1)S(1)}, u32[]{:S(2)}, u32[]{:S(2)}) %collective-permute-start.19) | collective-permute-done | bytes 524320 | tf_op jit(solution)/shard_map/ppermute | solution.py:381
  140.3 11.2 %collective-permute-done.20.refs_5_ = bf16[1024,256]{1,0:T(8,128)(2,1)S(1)} collective-permute-done((bf16[1024,256]{1,0:T(8,128)(2,1)S(1)}, bf16[1024,256]{1,0:T(8,128)(2,1)S(1)}, u32[]{:S(2)}, u32[]{:S(2)}) %collective-permute-start.20) | collective-permute-done | bytes 524320 | tf_op jit(solution)/shard_map/ppermute | solution.py:381
  154.1 4.2 shard_map.80
  158.4 2.4 collective-permute-done.refs_1_
  165.9 8.1 %collective-permute-done.22.refs_7_ = bf16[1024,256]{1,0:T(8,128)(2,1)} collective-permute-done((bf16[1024,256]{1,0:T(8,128)(2,1)S(1)}, bf16[1024,256]{1,0:T(8,128)(2,1)}, u32[]{:S(2)}, u32[]{:S(2)}) %collective-permute-start.22) | collective-permute-done | bytes 524320 | tf_op jit(solution)/shard_map/ppermute | solution.py:381
  175.8 14.9 %shard_map.83 = (bf16[512,2048]{1,0:T(8,128)(2,1)}, f32[512,2048]{1,0:T(8,128)}) custom-call(s32[2]{0:T(128)} %pad_add_fusion.at_ref, bf16[1024,256]{1,0:T(8,128)(2,1)} %get-tuple-element.65.refs_0_, bf16[1024,256]{1,0:T(8,128)(2,1)} %copy-done.44, bf16[1024,256]{1,0:T(8,128)(2,1)} %copy-done.45, bf16[1024,256]{1,0:T(8,128)(2,1)} %copy-done.46, ...), custom_call_target="tpu_custom_call" | custom-call | flops 8589934592 | bytes 20971520 | tf_op jit(solution)/shard_map/pallas_call | solution.py:110
  196.4 6.3 %collective-permute-done.3.refs_4_ = bf16[512,256]{1,0:T(8,128)(2,1)} collective-permute-done((bf16[512,256]{1,0:T(8,128)(2,1)}, bf16[512,256]{1,0:T(8,128)(2,1)}, u32[]{:S(2)}, u32[]{:S(2)}) %collective-permute-start.3) | collective-permute-done | bytes 262176 | tf_op jit(solution)/shard_map/ppermute | solution.py:381
  202.8 5.5 %collective-permute-done.31.refs_4_ = bf16[512,256]{1,0:T(8,128)(2,1)S(1)} collective-permute-done((bf16[512,256]{1,0:T(8,128)(2,1)S(1)}, bf16[512,256]{1,0:T(8,128)(2,1)S(1)}, u32[]{:S(2)}, u32[]{:S(2)}) %collective-permute-start.31) | collective-permute-done | bytes 262176 | tf_op jit(solution)/shard_map/ppermute | solution.py:381
  208.3 5.6 %collective-permute-done.32.refs_5_ = bf16[512,256]{1,0:T(8,128)(2,1)S(1)} collective-permute-done((bf16[512,256]{1,0:T(8,128)(2,1)S(1)}, bf16[512,256]{1,0:T(8,128)(2,1)S(1)}, u32[]{:S(2)}, u32[]{:S(2)}) %collective-permute-start.32) | collective-permute-done | bytes 262176 | tf_op jit(solution)/shard_map/ppermute | solution.py:381
  213.9 5.7 %collective-permute-done.4.refs_5_ = bf16[512,256]{1,0:T(8,128)(2,1)} collective-permute-done((bf16[512,256]{1,0:T(8,128)(2,1)}, bf16[512,256]{1,0:T(8,128)(2,1)}, u32[]{:S(2)}, u32[]{:S(2)}) %collective-permute-start.4) | collective-permute-done | bytes 262176 | tf_op jit(solution)/shard_map/ppermute | solution.py:381
  219.6 5.5 %collective-permute-done.33.refs_6_ = bf16[512,256]{1,0:T(8,128)(2,1)S(1)} collective-permute-done((bf16[512,256]{1,0:T(8,128)(2,1)S(1)}, bf16[512,256]{1,0:T(8,128)(2,1)S(1)}, u32[]{:S(2)}, u32[]{:S(2)}) %collective-permute-start.33) | collective-permute-done | bytes 262176 | tf_op jit(solution)/shard_map/ppermute | solution.py:381
  225.1 5.7 %collective-permute-done.34.refs_7_ = bf16[512,256]{1,0:T(8,128)(2,1)} collective-permute-done((bf16[512,256]{1,0:T(8,128)(2,1)S(1)}, bf16[512,256]{1,0:T(8,128)(2,1)}, u32[]{:S(2)}, u32[]{:S(2)}) %collective-permute-start.34) | collective-permute-done | bytes 262176 | tf_op jit(solution)/shard_map/ppermute | solution.py:381
  230.9 6.3 %shard_map.86 = (bf16[256,2048]{1,0:T(8,128)(2,1)}, f32[256,2048]{1,0:T(8,128)}) custom-call(s32[2]{0:T(128)} %pad_add_fusion.at_ref, bf16[512,256]{1,0:T(8,128)(2,1)} %get-tuple-element.73.refs_0_, bf16[512,256]{1,0:T(8,128)(2,1)} %copy-done.25, bf16[512,256]{1,0:T(8,128)(2,1)} %copy-done.26, bf16[512,256]{1,0:T(8,128)(2,1)} %copy-done.27, ...), custom_call_target="tpu_custom_call" | custom-call | flops 2147483648 | bytes 8388608 | tf_op jit(solution)/shard_map/pallas_call | solution.py:110
  237.2 6.3 %shard_map.87 = (bf16[256,2048]{1,0:T(8,128)(2,1)}, f32[256,2048]{1,0:T(8,128)}) custom-call(s32[2]{0:T(128)} %pad_add_fusion.at_ref, bf16[512,256]{1,0:T(8,128)(2,1)} %get-tuple-element.73.refs_0_, bf16[512,256]{1,0:T(8,128)(2,1)} %copy-done.25, bf16[512,256]{1,0:T(8,128)(2,1)} %copy-done.26, ...), custom_call_target="tpu_custom_call", output_to_operand_aliasing={{0}: (10, {}), {1}: (11, {})} | custom-call | flops 2147483648 | bytes 8388608 | tf_op jit(solution)/shard_map/pallas_call | solution.py:110
  243.5 10.1 %shard_map.77 = (bf16[256,2048]{1,0:T(8,128)(2,1)}, f32[256,2048]{1,0:T(8,128)}) custom-call(s32[2]{0:T(128)} %pad_add_fusion.at_ref, bf16[512,256]{1,0:T(8,128)(2,1)} %get-tuple-element.55.refs_0_, bf16[512,256]{1,0:T(8,128)(2,1)} %copy-done.49, bf16[512,256]{1,0:T(8,128)(2,1)} %copy-done.50, bf16[512,256]{1,0:T(8,128)(2,1)} %collective-permute-done.2.refs_3_, ...), custom_call_target="tpu_custom_call" | custom-call | flops 4294967296 | bytes 14680064 | tf_op jit(solution)/shard_map/pallas_call | solution.py:110
  254.7 7.8 %shard_map.81 = (bf16[4,128,1024]{2,1,0:T(8,128)(2,1)}, bf16[4,128,1024]{2,1,0:T(8,128)(2,1)}) custom-call(s32[3]{0:T(128)} %pad_add_fusion.1.at_ref, bf16[4,1024,1024]{2,1,0:T(8,128)(2,1)} %bitcast.18, bf16[2,1024,1024]{2,1,0:T(8,128)(2,1)} %collective-permute-done.10.got_ref.refs_1_, bf16[1024,1024]{1,0:T(8,128)(2,1)} %collective-permute-done.11.refs_2_), custom_call_target="tpu_custom_call" | custom-call | flops 3145728 | bytes 8388608 | tf_op jit(solution)/shard_map/pallas_call | solution.py:347
  265.4 2.8 shard_map.84
  272.3 2.1 shard_map.78
  274.9 30.7 %collective-permute-done.36.refs_0_ = bf16[128,2048]{1,0:T(8,128)(2,1)S(1)} collective-permute-done((bf16[128,2048]{1,0:T(8,128)(2,1)}, bf16[128,2048]{1,0:T(8,128)(2,1)S(1)}, u32[]{:S(2)}, u32[]{:S(2)}) %collective-permute-start.36) | collective-permute-done | bytes 524320 | tf_op jit(solution)/shard_map/ppermute | solution.py:384
  306.7 3.3 shard_map.89
  311.1 4.5 shard_map.85
  316.7 3.3 collective-permute-start.26
  321.5 3.0 collective-permute-start.39
  324.5 3.3 shard_map.82
  327.8 18.3 %collective-permute-done.38.refs_2_ = bf16[32,2048]{1,0:T(8,128)(2,1)S(1)} collective-permute-done((bf16[32,2048]{1,0:T(8,128)(2,1)S(1)}, bf16[32,2048]{1,0:T(8,128)(2,1)S(1)}, u32[]{:S(2)}, u32[]{:S(2)}) %collective-permute-start.38) | collective-permute-done | bytes 131104 | tf_op jit(solution)/shard_map/ppermute | solution.py:381
  348.2 3.4 collective-permute-start.14
  351.6 5.1 %shard_map.90 = (f32[128,8192]{1,0:T(8,128)}, f32[128,8192]{1,0:T(8,128)}, bf16[32,2048]{1,0:T(8,128)(2,1)}, bf16[32,2048]{1,0:T(8,128)(2,1)}, bf16[32,2048]{1,0:T(8,128)(2,1)}, /*index=5*/bf16[32,2048]{1,0:T(8,128)(2,1)}) custom-call(s32[2]{0:T(128)} %pad_add_fusion.at_ref, bf16[32,2048]{1,0:T(8,128)(2,1)} %get-tuple-element.79.refs_0_, ...), custom_call_target="tpu_custom_call" | custom-call | flops 2097152 | bytes 5242880 | tf_op jit(solution)/shard_map/pallas_call | solution.py:149
  359.5 6.4 %shard_map.91 = (f32[128,8192]{1,0:T(8,128)}, f32[128,8192]{1,0:T(8,128)}, bf16[64,2048]{1,0:T(8,128)(2,1)}, bf16[64,2048]{1,0:T(8,128)(2,1)}, bf16[64,2048]{1,0:T(8,128)(2,1)}, /*index=5*/bf16[64,2048]{1,0:T(8,128)(2,1)}) custom-call(s32[2]{0:T(128)} %pad_add_fusion.at_ref, ...), custom_call_target="tpu_custom_call", output_to_operand_aliasing={{0}: (7, {}), {1}: (8, {})} | custom-call | flops 4194304 | bytes 10485760 | tf_op jit(solution)/shard_map/pallas_call | solution.py:149
  366.1 2.5 collective-permute-start.51
  373.2 4.9 %shard_map.92 = (f32[128,8192]{1,0:T(8,128)}, f32[128,8192]{1,0:T(8,128)}, bf16[32,2048]{1,0:T(8,128)(2,1)}, bf16[32,2048]{1,0:T(8,128)(2,1)}, bf16[32,2048]{1,0:T(8,128)(2,1)}, /*index=5*/bf16[32,2048]{1,0:T(8,128)(2,1)}) custom-call(s32[2]{0:T(128)} %pad_add_fusion.at_ref, ...), custom_call_target="tpu_custom_call", output_to_operand_aliasing={{0}: (7, {}), {1}: (8, {})} | custom-call | flops 2097152 | bytes 5242880 | tf_op jit(solution)/shard_map/pallas_call | solution.py:149
  378.1 18.4 %collective-permute-done.61.refs_4_.refs_5_ = bf16[32,2048]{1,0:T(8,128)(2,1)S(1)} collective-permute-done((bf16[32,2048]{1,0:T(8,128)(2,1)S(1)}, bf16[32,2048]{1,0:T(8,128)(2,1)S(1)}, u32[]{:S(2)}, u32[]{:S(2)}) %collective-permute-start.61) | collective-permute-done | bytes 131104 | tf_op jit(solution)/shard_map/ppermute | solution.py:381
  397.2 2.6 shard_map.95
  401.2 3.0 shard_map.94
  406.2 3.1 collective-permute-start.41
  409.3 2.5 collective-permute-start.42
  411.8 4.5 collective-permute-done.41.refs_4_.refs_5_
  417.1 2.6 shard_map.93
  423.7 4.8 %collective-permute-done.44.refs_2_ = bf16[4,32,1024]{2,1,0:T(8,128)(2,1)S(1)} collective-permute-done((bf16[4,32,1024]{2,1,0:T(8,128)(2,1)}, bf16[4,32,1024]{2,1,0:T(8,128)(2,1)S(1)}, u32[]{:S(2)}, u32[]{:S(2)}) %collective-permute-start.44) | collective-permute-done | bytes 262176 | tf_op jit(solution)/shard_map/ppermute | solution.py:378
  430.3 15.9 %collective-permute-done.68.refs_6_ = bf16[4,32,1024]{2,1,0:T(8,128)(2,1)S(1)} collective-permute-done((bf16[4,32,1024]{2,1,0:T(8,128)(2,1)S(1)}, bf16[4,32,1024]{2,1,0:T(8,128)(2,1)S(1)}, u32[]{:S(2)}, u32[]{:S(2)}) %collective-permute-start.68) | collective-permute-done | bytes 262176 | tf_op jit(solution)/shard_map/ppermute | solution.py:384
  449.4 13.0 %collective-permute-done.48.refs_6_ = bf16[4,32,1024]{2,1,0:T(8,128)(2,1)} collective-permute-done((bf16[4,32,1024]{2,1,0:T(8,128)(2,1)S(1)}, bf16[4,32,1024]{2,1,0:T(8,128)(2,1)}, u32[]{:S(2)}, u32[]{:S(2)}) %collective-permute-start.48) | collective-permute-done | bytes 262176 | tf_op jit(solution)/shard_map/ppermute | solution.py:384
  465.7 3.5 shard_map.96.refs_8_
  469.3 4.9 %shard_map.97.refs_8_ = bf16[2,2,4,2,128,1024]{5,4,3,2,1,0:T(8,128)(2,1)} custom-call(s32[24]{0:T(128)} %stack.38.at_ref, bf16[4,64,1024]{2,1,0:T(8,128)(2,1)} %get-tuple-element.97.refs_0_, bf16[4,64,1024]{2,1,0:T(8,128)(2,1)} %copy-done.9, bf16[4,64,1024]{2,1,0:T(8,128)(2,1)} %copy-done.6, ...), custom_call_target="tpu_custom_call", output_to_operand_aliasing={{}: (9, {})} | custom-call | bytes 8388608 | tf_op jit(solution)/shard_map/pallas_call | solution.py:208
  474.2 3.5 shard_map.98
  (232 shorter events, 62.7 us)
Async XLA Ops:
  6.7 146.5 %collective-permute-start.10 = (bf16[2,1024,1024]{2,1,0:T(8,128)(2,1)}, bf16[2,1024,1024]{2,1,0:T(8,128)(2,1)}, u32[]{:S(2)}, u32[]{:S(2)}) collective-permute-start(bf16[2,1024,1024]{2,1,0:T(8,128)(2,1)} %shard_map.79), channel_id=1, source_target_pairs={{0,8},{8,0},{16,24},{24,16},{1,9},{9,1},{17,25},{25,17},{2,10},{10... | collective-permute-start | bytes 12582920 | tf_op jit(solution)/shard_map/ppermute | solution.py:387
  7.2 166.8 %collective-permute-start.7 = (bf16[2048,1024]{1,0:T(8,128)(2,1)}, bf16[2048,1024]{1,0:T(8,128)(2,1)}, u32[]{:S(2)}, u32[]{:S(2)}) collective-permute-start(bf16[2048,1024]{1,0:T(8,128)(2,1)} %bitcast.20), channel_id=1, source_target_pairs={{0,1},{1,0},{2,3},{3,2},{4,5},{5,4},{6,7},{7,6},{8,9},{9,8},{10,11... | collective-permute-start | bytes 12582920 | tf_op jit(solution)/shard_map/ppermute | solution.py:378
  15.1 97.2 %collective-permute-start.16 = (bf16[1024,256]{1,0:T(8,128)(2,1)}, bf16[1024,256]{1,0:T(8,128)(2,1)S(1)}, u32[]{:S(2)}, u32[]{:S(2)}) collective-permute-start(bf16[1024,256]{1,0:T(8,128)(2,1)} %get-tuple-element.66), channel_id=1, source_target_pairs={{0,1},{1,0},{2,3},{3,2},{4,5},{5,4},{6,7},{7,6},{8,9},{9,8},{10,11... | collective-permute-start | bytes 1572872 | tf_op jit(solution)/shard_map/ppermute | solution.py:378
  15.2 99.1 %collective-permute-start.17 = (bf16[1024,256]{1,0:T(8,128)(2,1)}, bf16[1024,256]{1,0:T(8,128)(2,1)S(1)}, u32[]{:S(2)}, u32[]{:S(2)}) collective-permute-start(bf16[1024,256]{1,0:T(8,128)(2,1)} %get-tuple-element.65.refs_0_), channel_id=1, source_target_pairs={{0,2},{1,3},{2,4},{3,5},{4,6},{5,7},{6,0},{7,1},{8,10},{9,11},{10,... | collective-permute-start | bytes 1572872 | tf_op jit(solution)/shard_map/ppermute | solution.py:381
  112.4 16.6 %collective-permute-start.18 = (bf16[1024,256]{1,0:T(8,128)(2,1)S(1)}, bf16[1024,256]{1,0:T(8,128)(2,1)S(1)}, u32[]{:S(2)}, u32[]{:S(2)}) collective-permute-start(bf16[1024,256]{1,0:T(8,128)(2,1)S(1)} %collective-permute-done.16.refs_1_), channel_id=1, source_target_pairs={{0,2},{1,3},{2,4},{3,5},{4,6},{5,7},{6,0},{7,1},{8,10},{9,11},{10,... | collective-permute-start | bytes 1572872 | tf_op jit(solution)/shard_map/ppermute | solution.py:381
  114.2 26.0 %collective-permute-start.19 = (bf16[1024,256]{1,0:T(8,128)(2,1)S(1)}, bf16[1024,256]{1,0:T(8,128)(2,1)S(1)}, u32[]{:S(2)}, u32[]{:S(2)}) collective-permute-start(bf16[1024,256]{1,0:T(8,128)(2,1)S(1)} %collective-permute-done.17.refs_2_), channel_id=1, source_target_pairs={{0,2},{1,3},{2,4},{3,5},{4,6},{5,7},{6,0},{7,1},{8,10},{9,11},{10,... | collective-permute-start | bytes 1572872 | tf_op jit(solution)/shard_map/ppermute | solution.py:381
  129.0 22.5 %collective-permute-start.20 = (bf16[1024,256]{1,0:T(8,128)(2,1)S(1)}, bf16[1024,256]{1,0:T(8,128)(2,1)S(1)}, u32[]{:S(2)}, u32[]{:S(2)}) collective-permute-start(bf16[1024,256]{1,0:T(8,128)(2,1)S(1)} %collective-permute-done.18.refs_3_), channel_id=1, source_target_pairs={{0,2},{1,3},{2,4},{3,5},{4,6},{5,7},{6,0},{7,1},{8,10},{9,11},{10,... | collective-permute-start | bytes 1572872 | tf_op jit(solution)/shard_map/ppermute | solution.py:381
  140.3 24.1 %collective-permute-start.21 = (bf16[1024,256]{1,0:T(8,128)(2,1)S(1)}, bf16[1024,256]{1,0:T(8,128)(2,1)}, u32[]{:S(2)}, u32[]{:S(2)}) collective-permute-start(bf16[1024,256]{1,0:T(8,128)(2,1)S(1)} %collective-permute-done.19.refs_4_), channel_id=1, source_target_pairs={{0,2},{1,3},{2,4},{3,5},{4,6},{5,7},{6,0},{7,1},{8,10},{9,11},{10,... | collective-permute-start | bytes 1572872 | tf_op jit(solution)/shard_map/ppermute | solution.py:381
  151.5 22.6 %collective-permute-start.22 = (bf16[1024,256]{1,0:T(8,128)(2,1)S(1)}, bf16[1024,256]{1,0:T(8,128)(2,1)}, u32[]{:S(2)}, u32[]{:S(2)}) collective-permute-start(bf16[1024,256]{1,0:T(8,128)(2,1)S(1)} %collective-permute-done.20.refs_5_), channel_id=1, source_target_pairs={{0,2},{1,3},{2,4},{3,5},{4,6},{5,7},{6,0},{7,1},{8,10},{9,11},{10,... | collective-permute-start | bytes 1572872 | tf_op jit(solution)/shard_map/ppermute | solution.py:381
  160.8 29.9 %collective-permute-start.1 = (bf16[512,256]{1,0:T(8,128)(2,1)}, bf16[512,256]{1,0:T(8,128)(2,1)S(1)}, u32[]{:S(2)}, u32[]{:S(2)}) collective-permute-start(bf16[512,256]{1,0:T(8,128)(2,1)} %get-tuple-element.55.refs_0_), channel_id=1, source_target_pairs={{0,2},{1,3},{2,4},{3,5},{4,6},{5,7},{6,0},{7,1},{8,10},{9,11},{10,... | collective-permute-start | bytes 786440 | tf_op jit(solution)/shard_map/ppermute | solution.py:381
  163.6 27.8 %collective-permute-start.29 = (bf16[512,256]{1,0:T(8,128)(2,1)S(1)}, bf16[512,256]{1,0:T(8,128)(2,1)S(1)}, u32[]{:S(2)}, u32[]{:S(2)}) collective-permute-start(bf16[512,256]{1,0:T(8,128)(2,1)S(1)} %copy-done.24), channel_id=1, source_target_pairs={{0,2},{1,3},{2,4},{3,5},{4,6},{5,7},{6,0},{7,1},{8,10},{9,11},{10,... | collective-permute-start | bytes 786440 | tf_op jit(solution)/shard_map/ppermute | solution.py:381
  164.4 28.5 %collective-permute-start.2 = (bf16[512,256]{1,0:T(8,128)(2,1)}, bf16[512,256]{1,0:T(8,128)(2,1)}, u32[]{:S(2)}, u32[]{:S(2)}) collective-permute-start(bf16[512,256]{1,0:T(8,128)(2,1)} %copy-done.49), channel_id=1, source_target_pairs={{0,2},{1,3},{2,4},{3,5},{4,6},{5,7},{6,0},{7,1},{8,10},{9,11},{10,... | collective-permute-start | bytes 786440 | tf_op jit(solution)/shard_map/ppermute | solution.py:381
  174.1 21.3 %collective-permute-start.30 = (bf16[512,256]{1,0:T(8,128)(2,1)S(1)}, bf16[512,256]{1,0:T(8,128)(2,1)S(1)}, u32[]{:S(2)}, u32[]{:S(2)}) collective-permute-start(bf16[512,256]{1,0:T(8,128)(2,1)S(1)} %collective-permute-done.28.refs_1_), channel_id=1, source_target_pairs={{0,2},{1,3},{2,4},{3,5},{4,6},{5,7},{6,0},{7,1},{8,10},{9,11},{10,... | collective-permute-start | bytes 786440 | tf_op jit(solution)/shard_map/ppermute | solution.py:381
  174.1 80.7 %collective-permute-start.11 = (bf16[1024,1024]{1,0:T(8,128)(2,1)}, bf16[1024,1024]{1,0:T(8,128)(2,1)}, u32[]{:S(2)}, u32[]{:S(2)}) collective-permute-start(bf16[1024,1024]{1,0:T(8,128)(2,1)} %shard_map.80), channel_id=1, source_target_pairs={{0,16},{8,24},{16,0},{24,8},{1,17},{9,25},{17,1},{25,9},{2,18},{10... | collective-permute-start | bytes 6291464 | tf_op jit(solution)/shard_map/ppermute | solution.py:384
  191.4 72.6 %collective-permute-start.23 = (bf16[512,2048]{1,0:T(8,128)(2,1)}, bf16[512,2048]{1,0:T(8,128)(2,1)S(1)}, u32[]{:S(2)}, u32[]{:S(2)}) collective-permute-start(bf16[512,2048]{1,0:T(8,128)(2,1)} %get-tuple-element.68), channel_id=1, source_target_pairs={{0,8},{8,0},{16,24},{24,16},{1,9},{9,1},{17,25},{25,17},{2,10},{10... | collective-permute-start | bytes 6291464 | tf_op jit(solution)/shard_map/ppermute | solution.py:387
  195.4 18.5 %collective-permute-start.32 = (bf16[512,256]{1,0:T(8,128)(2,1)S(1)}, bf16[512,256]{1,0:T(8,128)(2,1)S(1)}, u32[]{:S(2)}, u32[]{:S(2)}) collective-permute-start(bf16[512,256]{1,0:T(8,128)(2,1)S(1)} %collective-permute-done.30.refs_3_), channel_id=1, source_target_pairs={{0,2},{1,3},{2,4},{3,5},{4,6},{5,7},{6,0},{7,1},{8,10},{9,11},{10,... | collective-permute-start | bytes 786440 | tf_op jit(solution)/shard_map/ppermute | solution.py:381
  202.8 16.9 %collective-permute-start.4 = (bf16[512,256]{1,0:T(8,128)(2,1)}, bf16[512,256]{1,0:T(8,128)(2,1)}, u32[]{:S(2)}, u32[]{:S(2)}) collective-permute-start(bf16[512,256]{1,0:T(8,128)(2,1)} %collective-permute-done.2.refs_3_), channel_id=1, source_target_pairs={{0,2},{1,3},{2,4},{3,5},{4,6},{5,7},{6,0},{7,1},{8,10},{9,11},{10,... | collective-permute-start | bytes 786440 | tf_op jit(solution)/shard_map/ppermute | solution.py:381
  208.3 16.9 %collective-permute-start.33 = (bf16[512,256]{1,0:T(8,128)(2,1)S(1)}, bf16[512,256]{1,0:T(8,128)(2,1)S(1)}, u32[]{:S(2)}, u32[]{:S(2)}) collective-permute-start(bf16[512,256]{1,0:T(8,128)(2,1)S(1)} %collective-permute-done.31.refs_4_), channel_id=1, source_target_pairs={{0,2},{1,3},{2,4},{3,5},{4,6},{5,7},{6,0},{7,1},{8,10},{9,11},{10,... | collective-permute-start | bytes 786440 | tf_op jit(solution)/shard_map/ppermute | solution.py:381
  213.9 17.0 %collective-permute-start.34 = (bf16[512,256]{1,0:T(8,128)(2,1)S(1)}, bf16[512,256]{1,0:T(8,128)(2,1)}, u32[]{:S(2)}, u32[]{:S(2)}) collective-permute-start(bf16[512,256]{1,0:T(8,128)(2,1)S(1)} %collective-permute-done.32.refs_5_), channel_id=1, source_target_pairs={{0,2},{1,3},{2,4},{3,5},{4,6},{5,7},{6,0},{7,1},{8,10},{9,11},{10,... | collective-permute-start | bytes 786440 | tf_op jit(solution)/shard_map/ppermute | solution.py:381
  219.6 23.9 %collective-permute-start.5 = (bf16[512,256]{1,0:T(8,128)(2,1)}, bf16[512,256]{1,0:T(8,128)(2,1)}, u32[]{:S(2)}, u32[]{:S(2)}) collective-permute-start(bf16[512,256]{1,0:T(8,128)(2,1)} %collective-permute-done.3.refs_4_), channel_id=1, source_target_pairs={{0,2},{1,3},{2,4},{3,5},{4,6},{5,7},{6,0},{7,1},{8,10},{9,11},{10,... | collective-permute-start | bytes 786440 | tf_op jit(solution)/shard_map/ppermute | solution.py:381
  225.1 18.4 %collective-permute-start.6 = (bf16[512,256]{1,0:T(8,128)(2,1)}, bf16[512,256]{1,0:T(8,128)(2,1)}, u32[]{:S(2)}, u32[]{:S(2)}) collective-permute-start(bf16[512,256]{1,0:T(8,128)(2,1)} %collective-permute-done.4.refs_5_), channel_id=1, source_target_pairs={{0,2},{1,3},{2,4},{3,5},{4,6},{5,7},{6,0},{7,1},{8,10},{9,11},{10,... | collective-permute-start | bytes 786440 | tf_op jit(solution)/shard_map/ppermute | solution.py:381
  243.5 25.2 %collective-permute-start.35 = (bf16[256,2048]{1,0:T(8,128)(2,1)}, bf16[256,2048]{1,0:T(8,128)(2,1)}, u32[]{:S(2)}, u32[]{:S(2)}) collective-permute-start(bf16[256,2048]{1,0:T(8,128)(2,1)} %get-tuple-element.78), channel_id=1, source_target_pairs={{0,8},{8,0},{16,24},{24,16},{1,9},{9,1},{17,25},{25,17},{2,10},{10... | collective-permute-start | bytes 3145736 | tf_op jit(solution)/shard_map/ppermute | solution.py:387
  253.6 18.6 %collective-permute-start.8 = (bf16[256,2048]{1,0:T(8,128)(2,1)}, bf16[256,2048]{1,0:T(8,128)(2,1)}, u32[]{:S(2)}, u32[]{:S(2)}) collective-permute-start(bf16[256,2048]{1,0:T(8,128)(2,1)} %get-tuple-element.58), channel_id=1, source_target_pairs={{0,8},{8,0},{16,24},{24,16},{1,9},{9,1},{17,25},{25,17},{2,10},{10... | collective-permute-start | bytes 3145736 | tf_op jit(solution)/shard_map/ppermute | solution.py:387
  262.5 43.0 %collective-permute-start.12 = (bf16[4,128,1024]{2,1,0:T(8,128)(2,1)}, bf16[4,128,1024]{2,1,0:T(8,128)(2,1)S(1)}, u32[]{:S(2)}, u32[]{:S(2)}) collective-permute-start(bf16[4,128,1024]{2,1,0:T(8,128)(2,1)} %get-tuple-element.60), channel_id=1, source_target_pairs={{0,1},{1,0},{2,3},{3,2},{4,5},{5,4},{6,7},{7,6},{8,9},{9,8},{10,11... | collective-permute-start | bytes 3145736 | tf_op jit(solution)/shard_map/ppermute | solution.py:378
  268.1 41.9 %collective-permute-start.24 = (bf16[256,2048]{1,0:T(8,128)(2,1)}, bf16[256,2048]{1,0:T(8,128)(2,1)S(1)}, u32[]{:S(2)}, u32[]{:S(2)}) collective-permute-start(bf16[256,2048]{1,0:T(8,128)(2,1)} %shard_map.84), channel_id=1, source_target_pairs={{0,16},{8,24},{16,0},{24,8},{1,17},{9,25},{17,1},{25,9},{2,18},{10... | collective-permute-start | bytes 3145736 | tf_op jit(solution)/shard_map/ppermute | solution.py:384
  270.7 34.9 %collective-permute-start.36 = (bf16[128,2048]{1,0:T(8,128)(2,1)}, bf16[128,2048]{1,0:T(8,128)(2,1)S(1)}, u32[]{:S(2)}, u32[]{:S(2)}) collective-permute-start(bf16[128,2048]{1,0:T(8,128)(2,1)} %shard_map.88), channel_id=1, source_target_pairs={{0,16},{8,24},{16,0},{24,8},{1,17},{9,25},{17,1},{25,9},{2,18},{10... | collective-permute-start | bytes 1572872 | tf_op jit(solution)/shard_map/ppermute | solution.py:384
  274.4 46.7 %collective-permute-start.9 = (bf16[128,2048]{1,0:T(8,128)(2,1)}, bf16[128,2048]{1,0:T(8,128)(2,1)S(1)}, u32[]{:S(2)}, u32[]{:S(2)}) collective-permute-start(bf16[128,2048]{1,0:T(8,128)(2,1)} %shard_map.78), channel_id=1, source_target_pairs={{0,16},{8,24},{16,0},{24,8},{1,17},{9,25},{17,1},{25,9},{2,18},{10... | collective-permute-start | bytes 1572872 | tf_op jit(solution)/shard_map/ppermute | solution.py:384
  315.6 41.1 %collective-permute-start.25 = (bf16[64,2048]{1,0:T(8,128)(2,1)}, bf16[64,2048]{1,0:T(8,128)(2,1)S(1)}, u32[]{:S(2)}, u32[]{:S(2)}) collective-permute-start(bf16[64,2048]{1,0:T(8,128)(2,1)} %get-tuple-element.70), channel_id=1, source_target_pairs={{0,2},{1,3},{2,4},{3,5},{4,6},{5,7},{6,0},{7,1},{8,10},{9,11},{10,... | collective-permute-start | bytes 786440 | tf_op jit(solution)/shard_map/ppermute | solution.py:381
  316.7 40.2 %collective-permute-start.26 = (bf16[64,2048]{1,0:T(8,128)(2,1)}, bf16[64,2048]{1,0:T(8,128)(2,1)S(1)}, u32[]{:S(2)}, u32[]{:S(2)}) collective-permute-start(bf16[64,2048]{1,0:T(8,128)(2,1)} %get-tuple-element.71), channel_id=1, source_target_pairs={{0,4},{1,5},{2,6},{3,7},{4,0},{5,1},{6,2},{7,3},{8,12},{9,13},{10,... | collective-permute-start | bytes 786440 | tf_op jit(solution)/shard_map/ppermute | solution.py:381
  320.0 38.9 %collective-permute-start.27 = (bf16[64,2048]{1,0:T(8,128)(2,1)}, bf16[64,2048]{1,0:T(8,128)(2,1)S(1)}, u32[]{:S(2)}, u32[]{:S(2)}) collective-permute-start(bf16[64,2048]{1,0:T(8,128)(2,1)} %get-tuple-element.72), channel_id=1, source_target_pairs={{0,6},{1,7},{2,0},{3,1},{4,2},{5,3},{6,4},{7,5},{8,14},{9,15},{10,... | collective-permute-start | bytes 786440 | tf_op jit(solution)/shard_map/ppermute | solution.py:381
  321.1 25.0 %collective-permute-start.38 = (bf16[32,2048]{1,0:T(8,128)(2,1)S(1)}, bf16[32,2048]{1,0:T(8,128)(2,1)S(1)}, u32[]{:S(2)}, u32[]{:S(2)}) collective-permute-start(bf16[32,2048]{1,0:T(8,128)(2,1)S(1)} %copy-done.55), channel_id=1, source_target_pairs={{0,4},{1,5},{2,6},{3,7},{4,0},{5,1},{6,2},{7,3},{8,12},{9,13},{10,... | collective-permute-start | bytes 393224 | tf_op jit(solution)/shard_map/ppermute | solution.py:381
  321.5 26.7 %collective-permute-start.39 = (bf16[32,2048]{1,0:T(8,128)(2,1)S(1)}, bf16[32,2048]{1,0:T(8,128)(2,1)S(1)}, u32[]{:S(2)}, u32[]{:S(2)}) collective-permute-start(bf16[32,2048]{1,0:T(8,128)(2,1)S(1)} %copy-done.54), channel_id=1, source_target_pairs={{0,6},{1,7},{2,0},{3,1},{4,2},{5,3},{6,4},{7,5},{8,14},{9,15},{10,... | collective-permute-start | bytes 393224 | tf_op jit(solution)/shard_map/ppermute | solution.py:381
  346.1 20.0 %collective-permute-start.13 = (bf16[32,2048]{1,0:T(8,128)(2,1)}, bf16[32,2048]{1,0:T(8,128)(2,1)S(1)}, u32[]{:S(2)}, u32[]{:S(2)}) collective-permute-start(bf16[32,2048]{1,0:T(8,128)(2,1)} %get-tuple-element.62), channel_id=1, source_target_pairs={{0,2},{1,3},{2,4},{3,5},{4,6},{5,7},{6,0},{7,1},{8,10},{9,11},{10,... | collective-permute-start | bytes 393224 | tf_op jit(solution)/shard_map/ppermute | solution.py:381
  348.2 20.4 %collective-permute-start.14 = (bf16[32,2048]{1,0:T(8,128)(2,1)}, bf16[32,2048]{1,0:T(8,128)(2,1)S(1)}, u32[]{:S(2)}, u32[]{:S(2)}) collective-permute-start(bf16[32,2048]{1,0:T(8,128)(2,1)} %get-tuple-element.63), channel_id=1, source_target_pairs={{0,4},{1,5},{2,6},{3,7},{4,0},{5,1},{6,2},{7,3},{8,12},{9,13},{10,... | collective-permute-start | bytes 393224 | tf_op jit(solution)/shard_map/ppermute | solution.py:381
  366.0 34.3 %collective-permute-start.50 = (bf16[64,2048]{1,0:T(8,128)(2,1)}, bf16[64,2048]{1,0:T(8,128)(2,1)S(1)}, u32[]{:S(2)}, u32[]{:S(2)}) collective-permute-start(bf16[64,2048]{1,0:T(8,128)(2,1)} %get-tuple-element.94), channel_id=1, source_target_pairs={{0,2},{1,3},{2,4},{3,5},{4,6},{5,7},{6,0},{7,1},{8,10},{9,11},{10,... | collective-permute-start | bytes 786440 | tf_op jit(solution)/shard_map/ppermute | solution.py:381
  366.1 34.2 %collective-permute-start.51 = (bf16[64,2048]{1,0:T(8,128)(2,1)}, bf16[64,2048]{1,0:T(8,128)(2,1)S(1)}, u32[]{:S(2)}, u32[]{:S(2)}) collective-permute-start(bf16[64,2048]{1,0:T(8,128)(2,1)} %get-tuple-element.95), channel_id=1, source_target_pairs={{0,4},{1,5},{2,6},{3,7},{4,0},{5,1},{6,2},{7,3},{8,12},{9,13},{10,... | collective-permute-start | bytes 786440 | tf_op jit(solution)/shard_map/ppermute | solution.py:381
  368.7 31.7 %collective-permute-start.52 = (bf16[64,2048]{1,0:T(8,128)(2,1)}, bf16[64,2048]{1,0:T(8,128)(2,1)S(1)}, u32[]{:S(2)}, u32[]{:S(2)}) collective-permute-start(bf16[64,2048]{1,0:T(8,128)(2,1)} %get-tuple-element.96), channel_id=1, source_target_pairs={{0,6},{1,7},{2,0},{3,1},{4,2},{5,3},{6,4},{7,5},{8,14},{9,15},{10,... | collective-permute-start | bytes 786440 | tf_op jit(solution)/shard_map/ppermute | solution.py:381
  369.9 26.6 %collective-permute-start.61 = (bf16[32,2048]{1,0:T(8,128)(2,1)S(1)}, bf16[32,2048]{1,0:T(8,128)(2,1)S(1)}, u32[]{:S(2)}, u32[]{:S(2)}) collective-permute-start(bf16[32,2048]{1,0:T(8,128)(2,1)S(1)} %copy-done.52), channel_id=1, source_target_pairs={{0,4},{1,5},{2,6},{3,7},{4,0},{5,1},{6,2},{7,3},{8,12},{9,13},{10,... | collective-permute-start | bytes 393224 | tf_op jit(solution)/shard_map/ppermute | solution.py:381
  372.0 24.6 %collective-permute-start.62 = (bf16[32,2048]{1,0:T(8,128)(2,1)S(1)}, bf16[32,2048]{1,0:T(8,128)(2,1)S(1)}, u32[]{:S(2)}, u32[]{:S(2)}) collective-permute-start(bf16[32,2048]{1,0:T(8,128)(2,1)S(1)} %copy-done.51), channel_id=1, source_target_pairs={{0,6},{1,7},{2,0},{3,1},{4,2},{5,3},{6,4},{7,5},{8,14},{9,15},{10,... | collective-permute-start | bytes 393224 | tf_op jit(solution)/shard_map/ppermute | solution.py:381
  399.8 20.2 %collective-permute-start.64 = (bf16[4,32,1024]{2,1,0:T(8,128)(2,1)}, bf16[4,32,1024]{2,1,0:T(8,128)(2,1)S(1)}, u32[]{:S(2)}, u32[]{:S(2)}) collective-permute-start(bf16[4,32,1024]{2,1,0:T(8,128)(2,1)} %get-tuple-element.104), channel_id=1, source_target_pairs={{0,1},{1,0},{2,3},{3,2},{4,5},{5,4},{6,7},{7,6},{8,9},{9,8},{10,11... | collective-permute-start | bytes 786440 | tf_op jit(solution)/shard_map/ppermute | solution.py:378
  404.2 24.3 %collective-permute-start.54 = (bf16[4,64,1024]{2,1,0:T(8,128)(2,1)}, bf16[4,64,1024]{2,1,0:T(8,128)(2,1)S(1)}, u32[]{:S(2)}, u32[]{:S(2)}) collective-permute-start(bf16[4,64,1024]{2,1,0:T(8,128)(2,1)} %get-tuple-element.98), channel_id=1, source_target_pairs={{0,1},{1,0},{2,3},{3,2},{4,5},{5,4},{6,7},{7,6},{8,9},{9,8},{10,11... | collective-permute-start | bytes 1572872 | tf_op jit(solution)/shard_map/ppermute | solution.py:378
  421.7 27.7 %collective-permute-start.56 = (bf16[4,64,1024]{2,1,0:T(8,128)(2,1)}, bf16[4,64,1024]{2,1,0:T(8,128)(2,1)S(1)}, u32[]{:S(2)}, u32[]{:S(2)}) collective-permute-start(bf16[4,64,1024]{2,1,0:T(8,128)(2,1)} %get-tuple-element.97.refs_0_), channel_id=1, source_target_pairs={{0,16},{8,24},{16,0},{24,8},{1,17},{9,25},{17,1},{25,9},{2,18},{10... | collective-permute-start | bytes 1572872 | tf_op jit(solution)/shard_map/ppermute | solution.py:384
  422.0 24.2 %collective-permute-start.68 = (bf16[4,32,1024]{2,1,0:T(8,128)(2,1)S(1)}, bf16[4,32,1024]{2,1,0:T(8,128)(2,1)S(1)}, u32[]{:S(2)}, u32[]{:S(2)}) collective-permute-start(bf16[4,32,1024]{2,1,0:T(8,128)(2,1)S(1)} %collective-permute-done.64.refs_2_), channel_id=1, source_target_pairs={{0,16},{8,24},{16,0},{24,8},{1,17},{9,25},{17,1},{25,9},{2,18},{10... | collective-permute-start | bytes 786440 | tf_op jit(solution)/shard_map/ppermute | solution.py:384
  428.5 19.4 %collective-permute-start.65 = (bf16[4,32,1024]{2,1,0:T(8,128)(2,1)S(1)}, bf16[4,32,1024]{2,1,0:T(8,128)(2,1)S(1)}, u32[]{:S(2)}, u32[]{:S(2)}) collective-permute-start(bf16[4,32,1024]{2,1,0:T(8,128)(2,1)S(1)} %collective-permute-done.64.refs_2_), channel_id=1, source_target_pairs={{0,8},{8,0},{16,24},{24,16},{1,9},{9,1},{17,25},{25,17},{2,10},{10... | collective-permute-start | bytes 786440 | tf_op jit(solution)/shard_map/ppermute | solution.py:387
  428.5 33.9 %collective-permute-start.58 = (bf16[4,64,1024]{2,1,0:T(8,128)(2,1)S(1)}, bf16[4,64,1024]{2,1,0:T(8,128)(2,1)S(1)}, u32[]{:S(2)}, u32[]{:S(2)}) collective-permute-start(bf16[4,64,1024]{2,1,0:T(8,128)(2,1)S(1)} %collective-permute-done.54.refs_2_), channel_id=1, source_target_pairs={{0,16},{8,24},{16,0},{24,8},{1,17},{9,25},{17,1},{25,9},{2,18},{10... | collective-permute-start | bytes 1572872 | tf_op jit(solution)/shard_map/ppermute | solution.py:384
  430.1 18.5 %collective-permute-start.67 = (bf16[4,32,1024]{2,1,0:T(8,128)(2,1)S(1)}, bf16[4,32,1024]{2,1,0:T(8,128)(2,1)S(1)}, u32[]{:S(2)}, u32[]{:S(2)}) collective-permute-start(bf16[4,32,1024]{2,1,0:T(8,128)(2,1)S(1)} %collective-permute-done.66.refs_4_), channel_id=1, source_target_pairs={{0,8},{8,0},{16,24},{24,16},{1,9},{9,1},{17,25},{25,17},{2,10},{10... | collective-permute-start | bytes 786440 | tf_op jit(solution)/shard_map/ppermute | solution.py:387
  446.2 16.2 %collective-permute-start.48 = (bf16[4,32,1024]{2,1,0:T(8,128)(2,1)S(1)}, bf16[4,32,1024]{2,1,0:T(8,128)(2,1)}, u32[]{:S(2)}, u32[]{:S(2)}) collective-permute-start(bf16[4,32,1024]{2,1,0:T(8,128)(2,1)S(1)} %collective-permute-done.44.refs_2_), channel_id=1, source_target_pairs={{0,16},{8,24},{16,0},{24,8},{1,17},{9,25},{17,1},{25,9},{2,18},{10... | collective-permute-start | bytes 786440 | tf_op jit(solution)/shard_map/ppermute | solution.py:384
  448.0 16.1 %collective-permute-start.53 = (bf16[4,64,1024]{2,1,0:T(8,128)(2,1)}, bf16[4,64,1024]{2,1,0:T(8,128)(2,1)S(1)}, u32[]{:S(2)}, u32[]{:S(2)}) collective-permute-start(bf16[4,64,1024]{2,1,0:T(8,128)(2,1)} %get-tuple-element.97.refs_0_), channel_id=1, source_target_pairs={{0,8},{8,0},{16,24},{24,16},{1,9},{9,1},{17,25},{25,17},{2,10},{10... | collective-permute-start | bytes 1572872 | tf_op jit(solution)/shard_map/ppermute | solution.py:387
  (78 other events, 899.3 us)

commit v3 on v2

--- a/solution.py
+++ b/solution.py
@@ -17,7 +17,7 @@
     if rows % 128:
         return ((0, rows),)
     unit = rows // 4
-    return ((2 * unit, unit), (0, 2 * unit), (3 * unit, unit))
+    return ((0, unit), (unit, unit), (2 * unit, unit), (3 * unit, unit))
 
 
 f32, bf16 = jnp.float32, jnp.bfloat16
@@ -71,6 +71,7 @@
             scratch_shapes=[pltpu.VMEM((outer * size, span), bf16) for _ in range(inner) for _, size in strips if rows % 128],
         ),
         out_shape=[jax.ShapeDtypeStruct((reps * outer * size, tokens), bf16) for _ in range(inner) for _, size in strips],
+        compiler_params=pltpu.CompilerParams(vmem_limit_bytes=24 << 20),
         cost_estimate=pl.CostEstimate(flops=2 * tokens * width * span, bytes_accessed=4 * tokens * width, transcendentals=0),
     )(at, acts)
 
@@ -119,6 +120,7 @@
         ),
         out_shape=[jax.ShapeDtypeStruct((m // 2, inner * cols), d) for d in (bf16, f32)],
         input_output_aliases={1 + len(blocks) + count + i: i for i in range(len(held))},
+        compiler_params=pltpu.CompilerParams(vmem_limit_bytes=24 << 20),
         cost_estimate=pl.CostEstimate(
             flops=2 * m * tokens * count * cols, bytes_accessed=2 * (m * tokens + tokens * count * cols + 2 * m * count * cols), transcendentals=0
         ),
@@ -156,6 +158,7 @@
         ),
         out_shape=[shape, shape] + [jax.ShapeDtypeStruct((strip, span), bf16)] * outer,
         input_output_aliases={outer + 3 + i: i for i in range(len(held))},
+        compiler_params=pltpu.CompilerParams(vmem_limit_bytes=24 << 20),
         cost_estimate=pl.CostEstimate(flops=8 * outer * strip * span, bytes_accessed=20 * outer * strip * span, transcendentals=0),
     )(at, *parts, weights, momentum, *held)
     return out[:2], out[2:]
@@ -186,6 +189,7 @@
             out_specs=[pl.BlockSpec((outer, strip, cols), lambda i, at: (0, 0, 0))] * inner,
         ),
         out_shape=[jax.ShapeDtypeStruct((outer, strip, cols), bf16)] * inner,
+        compiler_params=pltpu.CompilerParams(vmem_limit_bytes=24 << 20),
         cost_estimate=pl.CostEstimate(flops=0, bytes_accessed=4 * outer * strip * span, transcendentals=0),
     )(at, *[p for p in parts for _ in range(inner)])
 
@@ -216,6 +220,7 @@
         ),
         out_shape=jax.ShapeDtypeStruct(shape, bf16),
         input_output_aliases={1 + len(found) + i: i for i in range(len(more))},
+        compiler_params=pltpu.CompilerParams(vmem_limit_bytes=24 << 20),
         cost_estimate=pl.CostEstimate(flops=0, bytes_accessed=4 * len(found) * found[0].size, transcendentals=0),
     )(at, *found, *more)
 
@@ -239,6 +244,7 @@
             pl.BlockSpec((m // high, width // 2), lambda j, i, k=k: (0, jnp.where(j == k, i, jnp.where(j < k, 0, 1)))) for k in range(high - 1)
         ],
         out_shape=[jax.ShapeDtypeStruct((m // high, width), bf16) for _ in range(high - 1)],
+        compiler_params=pltpu.CompilerParams(vmem_limit_bytes=24 << 20),
         cost_estimate=pl.CostEstimate(flops=m * width, bytes_accessed=8 * m * width * (high - 1) // high, transcendentals=0),
     )(here, away)
 
@@ -273,6 +279,7 @@
             out_specs=[pl.BlockSpec((strip, span), lambda i, at: (0, 0))] * outer,
         ),
         out_shape=[jax.ShapeDtypeStruct((strip, span), bf16)] * outer,
+        compiler_params=pltpu.CompilerParams(vmem_limit_bytes=24 << 20),
         cost_estimate=pl.CostEstimate(flops=4 * outer * strip * span, bytes_accessed=12 * outer * strip * span, transcendentals=0),
     )(at, here, away, *got, *drifts)
 
@@ -292,6 +299,7 @@
             out_specs=pl.BlockSpec((1, rows // 2, cols), lambda j, i, at: (j, i, 0)),
         ),
         out_shape=jax.ShapeDtypeStruct((count, rows, cols), array.dtype),
+        compiler_params=pltpu.CompilerParams(vmem_limit_bytes=24 << 20),
         cost_estimate=pl.CostEstimate(flops=0, bytes_accessed=4 * count * rows * cols, transcendentals=0),
     )(at, array)
 
@@ -321,6 +329,7 @@
             ],
         ),
         out_shape=[jax.ShapeDtypeStruct((rows, cols), bf16) for _ in range(count)],
+        compiler_params=pltpu.CompilerParams(vmem_limit_bytes=24 << 20),
         cost_estimate=pl.CostEstimate(flops=count * rows * cols, bytes_accessed=6 * count * rows * cols, transcendentals=0),
     )(at, mine, got)
 
@@ -360,6 +369,7 @@
             ],
         ),
         out_shape=[jax.ShapeDtypeStruct((outer, rows, cols), bf16) for _ in range(inner)],
+        compiler_params=pltpu.CompilerParams(vmem_limit_bytes=24 << 20),
         cost_estimate=pl.CostEstimate(flops=3 * length * cols, bytes_accessed=8 * length * cols, transcendentals=0),
     )(jnp.concatenate([place, at[:1]]), mine, got, *more)
 

time: 479 us -> 476 us (level)
  Pallas kernels: 114 us -> 77.5 us
  starting transfers between devices: 64.8 us -> 97.5 us
  local copies, waits for them, and re-layouts: 9.8 us -> 25.3 us
  waiting for transfers between devices: 286 us -> 274 us
    ppermute x36 -> x48, starting transfers between devices: 41.9 us -> 67.2 us  [over_z(): lax.ppermute(v, 'tp', [(a * inner + b, (a + k) % outer * inner + b) for a...]
    unnamed x112 -> x110, local copies, waits for them, and re-layouts: 8.55 us -> 25.1 us
    ppermute x10 -> x13, waiting for transfers between devices: 59.7 us -> 44.2 us  [over_y(): lax.ppermute(v, 'rep', [(a * pair + b, (a + k) % high * pair + b) for a i...]
    ppermute x8 -> x10, waiting for transfers between devices: 104 us -> 119 us  [over_x(): lax.ppermute(v, 'tp', [(a * inner + b, a * inner + (b + k) % inner) for a...]
    ppermute x36 -> x48, waiting for transfers between devices: 120 us -> 111 us  [over_z(): lax.ppermute(v, 'tp', [(a * inner + b, (a + k) % outer * inner + b) for a...]
    pallas_call x3 -> x4, Pallas kernels: 11.2 us -> 3.31 us  [full_sum(): pl.pallas_call(functools.partial(total_kernel, outer, inner, strip), grid...]
    pallas_call x3 -> x4, Pallas kernels: 6.98 us -> 1.13 us  [chip_sum(): pl.pallas_call(functools.partial(add_kernel, high), grid=(high - 1, 2), i...]
    pallas_call x3 -> x4, Pallas kernels: 8.13 us -> 2.33 us  [spread(): pl.pallas_call(functools.partial(spread_kernel, outer, inner), grid_spec=...]
  transfers between devices with their start and end apart: 70 -> 92, of which waited for: 22 -> 47; matrix products, arithmetic and copies ran while one was open for 1% -> 0% of each run, Pallas kernels for 22% -> 14%
where the time goes in v3:
time: 476 us
  waiting for transfers between devices  274 us (58%)
  starting transfers between devices  97.5 us (20%)
  Pallas kernels  77.5 us (16%)
  local copies, waits for them, and re-layouts  25.3 us (5%)
    ppermute x10, waiting for transfers between devices, over_x(): lax.ppermute(v, 'tp', [(a * inner + b, a * inner + (b + k) % inner) for a...  119 us
    ppermute x48, waiting for transfers between devices, over_z(): lax.ppermute(v, 'tp', [(a * inner + b, (a + k) % outer * inner + b) for a...  111 us
    ppermute x48, starting transfers between devices, over_z(): lax.ppermute(v, 'tp', [(a * inner + b, (a + k) % outer * inner + b) for a...  67.2 us
    ppermute x13, waiting for transfers between devices, over_y(): lax.ppermute(v, 'rep', [(a * pair + b, (a + k) % high * pair + b) for a i...  44.2 us
    pallas_call x5, Pallas kernels, partial_grad(): pl.pallas_call(functools.partial(dot_kernel, outer, inner, count), grid_s...  37 us
    unnamed x110, local copies, waits for them, and re-layouts  25.1 us
    ppermute x13, starting transfers between devices, over_y(): lax.ppermute(v, 'rep', [(a * pair + b, (a + k) % high * pair + b) for a i...  16.9 us
    pallas_call x4, Pallas kernels, outer_step(): pl.pallas_call(functools.partial(step_kernel, outer, reps), grid_spec=plt...  10.9 us
  transfers between devices with their start and end apart: 92, of which 47 were waited for; matrix products, arithmetic and copies ran while one was open for 0% of the time, Pallas kernels for 14%

profile of v3, /device:TPU:0, one launch (start us, length us, event | category | flops | bytes accessed | tf_op | source)
XLA Modules:
  0.0 475.8 jit_solution(3381724229958878155)
XLA Ops:
  0.7 3.4 copy-done
  4.1 3.0 shard_map.79
  14.4 92.9 %collective-permute-done.refs_1_ = bf16[512,256]{1,0:T(8,128)(2,1)S(1)} collective-permute-done((bf16[512,256]{1,0:T(8,128)(2,1)S(1)}, bf16[512,256]{1,0:T(8,128)(2,1)S(1)}, u32[]{:S(2)}, u32[]{:S(2)}) %collective-permute-start) | collective-permute-done | bytes 262176 | tf_op jit(solution)/shard_map/ppermute | solution.py:388
  109.4 3.6 collective-permute-done.16.refs_1_
  115.1 3.5 collective-permute-done.28.refs_1_
  129.7 5.3 %collective-permute-done.29.refs_2_ = bf16[512,256]{1,0:T(8,128)(2,1)S(1)} collective-permute-done((bf16[512,256]{1,0:T(8,128)(2,1)S(1)}, bf16[512,256]{1,0:T(8,128)(2,1)S(1)}, u32[]{:S(2)}, u32[]{:S(2)}) %collective-permute-start.29) | collective-permute-done | bytes 262176 | tf_op jit(solution)/shard_map/ppermute | solution.py:391
  135.7 4.9 %collective-permute-done.41.refs_2_ = bf16[512,256]{1,0:T(8,128)(2,1)S(1)} collective-permute-done((bf16[512,256]{1,0:T(8,128)(2,1)S(1)}, bf16[512,256]{1,0:T(8,128)(2,1)S(1)}, u32[]{:S(2)}, u32[]{:S(2)}) %collective-permute-start.41) | collective-permute-done | bytes 262176 | tf_op jit(solution)/shard_map/ppermute | solution.py:391
  141.3 4.9 %collective-permute-done.2.refs_3_ = bf16[512,256]{1,0:T(8,128)(2,1)S(1)} collective-permute-done((bf16[512,256]{1,0:T(8,128)(2,1)S(1)}, bf16[512,256]{1,0:T(8,128)(2,1)S(1)}, u32[]{:S(2)}, u32[]{:S(2)}) %collective-permute-start.2) | collective-permute-done | bytes 262176 | tf_op jit(solution)/shard_map/ppermute | solution.py:391
  146.3 5.7 %collective-permute-done.18.refs_3_ = bf16[512,256]{1,0:T(8,128)(2,1)} collective-permute-done((bf16[512,256]{1,0:T(8,128)(2,1)S(1)}, bf16[512,256]{1,0:T(8,128)(2,1)}, u32[]{:S(2)}, u32[]{:S(2)}) %collective-permute-start.18) | collective-permute-done | bytes 262176 | tf_op jit(solution)/shard_map/ppermute | solution.py:391
  152.0 5.5 %collective-permute-done.30.refs_3_ = bf16[512,256]{1,0:T(8,128)(2,1)S(1)} collective-permute-done((bf16[512,256]{1,0:T(8,128)(2,1)S(1)}, bf16[512,256]{1,0:T(8,128)(2,1)S(1)}, u32[]{:S(2)}, u32[]{:S(2)}) %collective-permute-start.30) | collective-permute-done | bytes 262176 | tf_op jit(solution)/shard_map/ppermute | solution.py:391
  158.3 4.8 %collective-permute-done.42.refs_3_ = bf16[512,256]{1,0:T(8,128)(2,1)S(1)} collective-permute-done((bf16[512,256]{1,0:T(8,128)(2,1)S(1)}, bf16[512,256]{1,0:T(8,128)(2,1)S(1)}, u32[]{:S(2)}, u32[]{:S(2)}) %collective-permute-start.42) | collective-permute-done | bytes 262176 | tf_op jit(solution)/shard_map/ppermute | solution.py:391
  163.8 4.9 %collective-permute-done.3.refs_4_ = bf16[512,256]{1,0:T(8,128)(2,1)S(1)} collective-permute-done((bf16[512,256]{1,0:T(8,128)(2,1)S(1)}, bf16[512,256]{1,0:T(8,128)(2,1)S(1)}, u32[]{:S(2)}, u32[]{:S(2)}) %collective-permute-start.3) | collective-permute-done | bytes 262176 | tf_op jit(solution)/shard_map/ppermute | solution.py:391
  169.4 4.9 %collective-permute-done.19.refs_4_ = bf16[512,256]{1,0:T(8,128)(2,1)S(1)} collective-permute-done((bf16[512,256]{1,0:T(8,128)(2,1)S(1)}, bf16[512,256]{1,0:T(8,128)(2,1)S(1)}, u32[]{:S(2)}, u32[]{:S(2)}) %collective-permute-start.19) | collective-permute-done | bytes 262176 | tf_op jit(solution)/shard_map/ppermute | solution.py:391
  174.3 5.6 %collective-permute-done.31.refs_4_ = bf16[512,256]{1,0:T(8,128)(2,1)S(1)} collective-permute-done((bf16[512,256]{1,0:T(8,128)(2,1)S(1)}, bf16[512,256]{1,0:T(8,128)(2,1)S(1)}, u32[]{:S(2)}, u32[]{:S(2)}) %collective-permute-start.31) | collective-permute-done | bytes 262176 | tf_op jit(solution)/shard_map/ppermute | solution.py:391
  180.0 5.6 %collective-permute-done.43.refs_4_ = bf16[512,256]{1,0:T(8,128)(2,1)S(1)} collective-permute-done((bf16[512,256]{1,0:T(8,128)(2,1)S(1)}, bf16[512,256]{1,0:T(8,128)(2,1)S(1)}, u32[]{:S(2)}, u32[]{:S(2)}) %collective-permute-start.43) | collective-permute-done | bytes 262176 | tf_op jit(solution)/shard_map/ppermute | solution.py:391
  185.6 5.6 %collective-permute-done.44.refs_5_ = bf16[512,256]{1,0:T(8,128)(2,1)S(1)} collective-permute-done((bf16[512,256]{1,0:T(8,128)(2,1)S(1)}, bf16[512,256]{1,0:T(8,128)(2,1)S(1)}, u32[]{:S(2)}, u32[]{:S(2)}) %collective-permute-start.44) | collective-permute-done | bytes 262176 | tf_op jit(solution)/shard_map/ppermute | solution.py:391
  192.8 3.4 copy-done.1
  202.5 5.5 %collective-permute-done.45.refs_6_ = bf16[512,256]{1,0:T(8,128)(2,1)S(1)} collective-permute-done((bf16[512,256]{1,0:T(8,128)(2,1)S(1)}, bf16[512,256]{1,0:T(8,128)(2,1)S(1)}, u32[]{:S(2)}, u32[]{:S(2)}) %collective-permute-start.45) | collective-permute-done | bytes 262176 | tf_op jit(solution)/shard_map/ppermute | solution.py:391
  208.0 5.6 %collective-permute-done.46.refs_7_ = bf16[512,256]{1,0:T(8,128)(2,1)S(1)} collective-permute-done((bf16[512,256]{1,0:T(8,128)(2,1)S(1)}, bf16[512,256]{1,0:T(8,128)(2,1)S(1)}, u32[]{:S(2)}, u32[]{:S(2)}) %collective-permute-start.46) | collective-permute-done | bytes 262176 | tf_op jit(solution)/shard_map/ppermute | solution.py:391
  215.5 4.8 %shard_map.89 = (bf16[256,2048]{1,0:T(8,128)(2,1)S(1)}, f32[256,2048]{1,0:T(8,128)S(1)}) custom-call(s32[2]{0:T(128)S(1)} %pad_add_fusion.at_ref, bf16[512,256]{1,0:T(8,128)(2,1)S(1)} %get-tuple-element.97.refs_0_, bf16[512,256]{1,0:T(8,128)(2,1)S(1)} %collective-permute-done.40.refs_1_, bf16[512,256]{1,0:T(8,128)(2,1)S(1)} %collective-permute-done.41.refs_2_, ...), custom_call_target="tpu_custom_call" | custom-call | flops 2147483648 | bytes 8388608 | tf_op jit(solution)/shard_map/pallas_call | solution.py:111
  220.4 4.5 collective-permute-done.21.refs_6_
  224.9 5.6 %collective-permute-done.22.refs_7_ = bf16[512,256]{1,0:T(8,128)(2,1)S(1)} collective-permute-done((bf16[512,256]{1,0:T(8,128)(2,1)}, bf16[512,256]{1,0:T(8,128)(2,1)S(1)}, u32[]{:S(2)}, u32[]{:S(2)}) %collective-permute-start.22) | collective-permute-done | bytes 262176 | tf_op jit(solution)/shard_map/ppermute | solution.py:391
  232.1 9.2 %shard_map.83 = (bf16[256,2048]{1,0:T(8,128)(2,1)}, f32[256,2048]{1,0:T(8,128)S(1)}) custom-call(s32[2]{0:T(128)S(1)} %pad_add_fusion.at_ref, bf16[512,256]{1,0:T(8,128)(2,1)S(1)} %copy-done.38, bf16[512,256]{1,0:T(8,128)(2,1)S(1)} %copy-done.40, bf16[512,256]{1,0:T(8,128)(2,1)S(1)} %copy-done.46, bf16[512,256]{1,0:T(8,128)(2,1)} %collective-permute-done.18.refs_3_, ...), custom_call_target="tpu_custom_call" | custom-call | flops 4294967296 | bytes 14680064 | tf_op jit(solution)/shard_map/pallas_call | solution.py:111
  241.8 10.2 %collective-permute-done.34.refs_7_ = bf16[512,256]{1,0:T(8,128)(2,1)S(1)} collective-permute-done((bf16[512,256]{1,0:T(8,128)(2,1)S(1)}, bf16[512,256]{1,0:T(8,128)(2,1)S(1)}, u32[]{:S(2)}, u32[]{:S(2)}) %collective-permute-start.34) | collective-permute-done | bytes 262176 | tf_op jit(solution)/shard_map/ppermute | solution.py:391
  252.0 9.1 %shard_map.86 = (bf16[256,2048]{1,0:T(8,128)(2,1)}, f32[256,2048]{1,0:T(8,128)S(1)}) custom-call(s32[2]{0:T(128)S(1)} %pad_add_fusion.at_ref, bf16[512,256]{1,0:T(8,128)(2,1)S(1)} %copy-done.32, bf16[512,256]{1,0:T(8,128)(2,1)S(1)} %copy-done.34, bf16[512,256]{1,0:T(8,128)(2,1)S(1)} %copy-done.42, bf16[512,256]{1,0:T(8,128)(2,1)S(1)} %copy-done.48, ...), custom_call_target="tpu_custom_call" | custom-call | flops 4294967296 | bytes 14680064 | tf_op jit(solution)/shard_map/pallas_call | solution.py:111
  261.1 4.8 %shard_map.90 = (bf16[256,2048]{1,0:T(8,128)(2,1)S(1)}, f32[256,2048]{1,0:T(8,128)S(1)}) custom-call(s32[2]{0:T(128)S(1)} %pad_add_fusion.at_ref, bf16[512,256]{1,0:T(8,128)(2,1)S(1)} %get-tuple-element.97.refs_0_, bf16[512,256]{1,0:T(8,128)(2,1)S(1)} %collective-permute-done.40.refs_1_, ...), custom_call_target="tpu_custom_call", output_to_operand_aliasing={{0}: (10, {}), {1}: (11, {})} | custom-call | flops 2147483648 | bytes 8388608 | tf_op jit(solution)/shard_map/pallas_call | solution.py:111
  266.5 9.1 %shard_map.77 = (bf16[256,2048]{1,0:T(8,128)(2,1)S(1)}, f32[256,2048]{1,0:T(8,128)S(1)}) custom-call(s32[2]{0:T(128)S(1)} %pad_add_fusion.at_ref, bf16[512,256]{1,0:T(8,128)(2,1)S(1)} %get-tuple-element.71.refs_0_, bf16[512,256]{1,0:T(8,128)(2,1)S(1)} %collective-permute-done.refs_1_, bf16[512,256]{1,0:T(8,128)(2,1)S(1)} %copy-done.30, ...), custom_call_target="tpu_custom_call" | custom-call | flops 4294967296 | bytes 14680064 | tf_op jit(solution)/shard_map/pallas_call | solution.py:111
  275.8 5.4 %shard_map.81 = (bf16[4,128,1024]{2,1,0:T(8,128)(2,1)S(1)}, bf16[4,128,1024]{2,1,0:T(8,128)(2,1)S(1)}) custom-call(s32[3]{0:T(128)S(1)} %pad_add_fusion.1.at_ref, bf16[4,1024,1024]{2,1,0:T(8,128)(2,1)S(1)} %bitcast.20, bf16[2,1024,1024]{2,1,0:T(8,128)(2,1)} %collective-permute-done.10.got_ref.refs_1_, bf16[1024,1024]{1,0:T(8,128)(2,1)S(1)} %collective-permute-done.11.refs_2_), custom_call_target="tpu_custom_call" | custom-call | flops 3145728 | bytes 8388608 | tf_op jit(solution)/shard_map/pallas_call | solution.py:356
  288.2 9.7 %collective-permute-done.24.refs_0_ = bf16[128,2048]{1,0:T(8,128)(2,1)S(1)} collective-permute-done((bf16[128,2048]{1,0:T(8,128)(2,1)S(1)}, bf16[128,2048]{1,0:T(8,128)(2,1)S(1)}, u32[]{:S(2)}, u32[]{:S(2)}) %collective-permute-start.24) | collective-permute-done | bytes 524320 | tf_op jit(solution)/shard_map/ppermute | solution.py:394
  297.9 8.9 %collective-permute-done.12.refs_2_ = bf16[4,128,1024]{2,1,0:T(8,128)(2,1)S(1)} collective-permute-done((bf16[4,128,1024]{2,1,0:T(8,128)(2,1)S(1)}, bf16[4,128,1024]{2,1,0:T(8,128)(2,1)S(1)}, u32[]{:S(2)}, u32[]{:S(2)}) %collective-permute-start.12) | collective-permute-done | bytes 1048608 | tf_op jit(solution)/shard_map/ppermute | solution.py:388
  310.0 2.9 collective-permute-start.38
  312.9 7.4 %collective-permute-done.48.refs_0_ = bf16[128,2048]{1,0:T(8,128)(2,1)S(1)} collective-permute-done((bf16[128,2048]{1,0:T(8,128)(2,1)S(1)}, bf16[128,2048]{1,0:T(8,128)(2,1)S(1)}, u32[]{:S(2)}, u32[]{:S(2)}) %collective-permute-start.48) | collective-permute-done | bytes 524320 | tf_op jit(solution)/shard_map/ppermute | solution.py:394
  322.9 7.9 %collective-permute-done.9.refs_0_ = bf16[128,2048]{1,0:T(8,128)(2,1)S(1)} collective-permute-done((bf16[128,2048]{1,0:T(8,128)(2,1)S(1)}, bf16[128,2048]{1,0:T(8,128)(2,1)S(1)}, u32[]{:S(2)}, u32[]{:S(2)}) %collective-permute-start.9) | collective-permute-done | bytes 524320 | tf_op jit(solution)/shard_map/ppermute | solution.py:394
  339.6 4.9 %collective-permute-done.50.refs_2_ = bf16[32,2048]{1,0:T(8,128)(2,1)S(1)} collective-permute-done((bf16[32,2048]{1,0:T(8,128)(2,1)S(1)}, bf16[32,2048]{1,0:T(8,128)(2,1)S(1)}, u32[]{:S(2)}, u32[]{:S(2)}) %collective-permute-start.50) | collective-permute-done | bytes 131104 | tf_op jit(solution)/shard_map/ppermute | solution.py:391
  344.5 2.9 collective-permute-start.14
  347.4 7.4 %collective-permute-start.15 = (bf16[32,2048]{1,0:T(8,128)(2,1)S(1)}, bf16[32,2048]{1,0:T(8,128)(2,1)S(1)}, u32[]{:S(2)}, u32[]{:S(2)}) collective-permute-start(bf16[32,2048]{1,0:T(8,128)(2,1)S(1)} %get-tuple-element.80), channel_id=1, source_target_pairs={{0,6},{1,7},{2,0},{3,1},{4,2},{5,3},{6,4},{7,5},{8,14},{9,15},{10,... | collective-permute-start | bytes 393224 | tf_op jit(solution)/shard_map/ppermute | solution.py:391
  360.3 2.7 shard_map.95
  363.0 2.7 shard_map.96
  369.4 2.9 collective-permute-start.83
  379.7 7.9 %collective-permute-start.72 = (bf16[32,2048]{1,0:T(8,128)(2,1)S(1)}, bf16[32,2048]{1,0:T(8,128)(2,1)S(1)}, u32[]{:S(2)}, u32[]{:S(2)}) collective-permute-start(bf16[32,2048]{1,0:T(8,128)(2,1)S(1)} %get-tuple-element.126), channel_id=1, source_target_pairs={{0,2},{1,3},{2,4},{3,5},{4,6},{5,7},{6,0},{7,1},{8,10},{9,11},{10,... | collective-permute-start | bytes 393224 | tf_op jit(solution)/shard_map/ppermute | solution.py:391
  390.0 9.0 %collective-permute-start.74 = (bf16[32,2048]{1,0:T(8,128)(2,1)S(1)}, bf16[32,2048]{1,0:T(8,128)(2,1)S(1)}, u32[]{:S(2)}, u32[]{:S(2)}) collective-permute-start(bf16[32,2048]{1,0:T(8,128)(2,1)S(1)} %get-tuple-element.128), channel_id=1, source_target_pairs={{0,6},{1,7},{2,0},{3,1},{4,2},{5,3},{6,4},{7,5},{8,14},{9,15},{10,... | collective-permute-start | bytes 393224 | tf_op jit(solution)/shard_map/ppermute | solution.py:391
  403.9 2.8 collective-permute-start.54
  407.9 4.4 collective-permute-done.53.refs_4_.refs_5_
  417.1 4.1 collective-permute-done.76.refs_2_
  434.6 5.6 %collective-permute-done.90.refs_6_ = bf16[4,32,1024]{2,1,0:T(8,128)(2,1)S(1)} collective-permute-done((bf16[4,32,1024]{2,1,0:T(8,128)(2,1)S(1)}, bf16[4,32,1024]{2,1,0:T(8,128)(2,1)S(1)}, u32[]{:S(2)}, u32[]{:S(2)}) %collective-permute-start.90) | collective-permute-done | bytes 262176 | tf_op jit(solution)/shard_map/ppermute | solution.py:394
  452.6 3.2 collective-permute-done.60.refs_6_
  469.4 2.9 shard_map.103.refs_8_
  472.4 3.2 shard_map.104
  (281 shorter events, 129.4 us)
Async XLA Ops:
  7.1 184.1 %collective-permute-start.10 = (bf16[2,1024,1024]{2,1,0:T(8,128)(2,1)}, bf16[2,1024,1024]{2,1,0:T(8,128)(2,1)}, u32[]{:S(2)}, u32[]{:S(2)}) collective-permute-start(bf16[2,1024,1024]{2,1,0:T(8,128)(2,1)} %shard_map.79), channel_id=1, source_target_pairs={{0,8},{8,0},{16,24},{24,16},{1,9},{9,1},{17,25},{25,17},{2,10},{10... | collective-permute-start | bytes 12582920 | tf_op jit(solution)/shard_map/ppermute | solution.py:397
  7.6 222.9 %collective-permute-start.7 = (bf16[2048,1024]{1,0:T(8,128)(2,1)}, bf16[2048,1024]{1,0:T(8,128)(2,1)}, u32[]{:S(2)}, u32[]{:S(2)}) collective-permute-start(bf16[2048,1024]{1,0:T(8,128)(2,1)} %bitcast.13.refs_8_), channel_id=1, source_target_pairs={{0,1},{1,0},{2,3},{3,2},{4,5},{5,4},{6,7},{7,6},{8,9},{9,8},{10,11... | collective-permute-start | bytes 12582920 | tf_op jit(solution)/shard_map/ppermute | solution.py:388
  12.2 95.1 %collective-permute-start = (bf16[512,256]{1,0:T(8,128)(2,1)S(1)}, bf16[512,256]{1,0:T(8,128)(2,1)S(1)}, u32[]{:S(2)}, u32[]{:S(2)}) collective-permute-start(bf16[512,256]{1,0:T(8,128)(2,1)S(1)} %get-tuple-element.72), channel_id=1, source_target_pairs={{0,1},{1,0},{2,3},{3,2},{4,5},{5,4},{6,7},{7,6},{8,9},{9,8},{10,11... | collective-permute-start | bytes 786440 | tf_op jit(solution)/shard_map/ppermute | solution.py:388
  12.3 100.7 %collective-permute-start.16 = (bf16[512,256]{1,0:T(8,128)(2,1)S(1)}, bf16[512,256]{1,0:T(8,128)(2,1)S(1)}, u32[]{:S(2)}, u32[]{:S(2)}) collective-permute-start(bf16[512,256]{1,0:T(8,128)(2,1)S(1)} %get-tuple-element.82), channel_id=1, source_target_pairs={{0,1},{1,0},{2,3},{3,2},{4,5},{5,4},{6,7},{7,6},{8,9},{9,8},{10,11... | collective-permute-start | bytes 786440 | tf_op jit(solution)/shard_map/ppermute | solution.py:388
  14.3 104.3 %collective-permute-start.28 = (bf16[512,256]{1,0:T(8,128)(2,1)S(1)}, bf16[512,256]{1,0:T(8,128)(2,1)S(1)}, u32[]{:S(2)}, u32[]{:S(2)}) collective-permute-start(bf16[512,256]{1,0:T(8,128)(2,1)S(1)} %get-tuple-element.90), channel_id=1, source_target_pairs={{0,1},{1,0},{2,3},{3,2},{4,5},{5,4},{6,7},{7,6},{8,9},{9,8},{10,11... | collective-permute-start | bytes 786440 | tf_op jit(solution)/shard_map/ppermute | solution.py:388
  107.3 16.7 %collective-permute-start.40 = (bf16[512,256]{1,0:T(8,128)(2,1)S(1)}, bf16[512,256]{1,0:T(8,128)(2,1)S(1)}, u32[]{:S(2)}, u32[]{:S(2)}) collective-permute-start(bf16[512,256]{1,0:T(8,128)(2,1)S(1)} %get-tuple-element.98), channel_id=1, source_target_pairs={{0,1},{1,0},{2,3},{3,2},{4,5},{5,4},{6,7},{7,6},{8,9},{9,8},{10,11... | collective-permute-start | bytes 786440 | tf_op jit(solution)/shard_map/ppermute | solution.py:388
  128.4 17.9 %collective-permute-start.2 = (bf16[512,256]{1,0:T(8,128)(2,1)S(1)}, bf16[512,256]{1,0:T(8,128)(2,1)S(1)}, u32[]{:S(2)}, u32[]{:S(2)}) collective-permute-start(bf16[512,256]{1,0:T(8,128)(2,1)S(1)} %collective-permute-done.refs_1_), channel_id=1, source_target_pairs={{0,2},{1,3},{2,4},{3,5},{4,6},{5,7},{6,0},{7,1},{8,10},{9,11},{10,... | collective-permute-start | bytes 786440 | tf_op jit(solution)/shard_map/ppermute | solution.py:391
  135.0 17.0 %collective-permute-start.18 = (bf16[512,256]{1,0:T(8,128)(2,1)S(1)}, bf16[512,256]{1,0:T(8,128)(2,1)}, u32[]{:S(2)}, u32[]{:S(2)}) collective-permute-start(bf16[512,256]{1,0:T(8,128)(2,1)S(1)} %collective-permute-done.16.refs_1_), channel_id=1, source_target_pairs={{0,2},{1,3},{2,4},{3,5},{4,6},{5,7},{6,0},{7,1},{8,10},{9,11},{10,... | collective-permute-start | bytes 786440 | tf_op jit(solution)/shard_map/ppermute | solution.py:391
  140.6 16.9 %collective-permute-start.30 = (bf16[512,256]{1,0:T(8,128)(2,1)S(1)}, bf16[512,256]{1,0:T(8,128)(2,1)S(1)}, u32[]{:S(2)}, u32[]{:S(2)}) collective-permute-start(bf16[512,256]{1,0:T(8,128)(2,1)S(1)} %collective-permute-done.28.refs_1_), channel_id=1, source_target_pairs={{0,2},{1,3},{2,4},{3,5},{4,6},{5,7},{6,0},{7,1},{8,10},{9,11},{10,... | collective-permute-start | bytes 786440 | tf_op jit(solution)/shard_map/ppermute | solution.py:391
  146.2 16.9 %collective-permute-start.42 = (bf16[512,256]{1,0:T(8,128)(2,1)S(1)}, bf16[512,256]{1,0:T(8,128)(2,1)S(1)}, u32[]{:S(2)}, u32[]{:S(2)}) collective-permute-start(bf16[512,256]{1,0:T(8,128)(2,1)S(1)} %collective-permute-done.40.refs_1_), channel_id=1, source_target_pairs={{0,2},{1,3},{2,4},{3,5},{4,6},{5,7},{6,0},{7,1},{8,10},{9,11},{10,... | collective-permute-start | bytes 786440 | tf_op jit(solution)/shard_map/ppermute | solution.py:391
  152.0 16.7 %collective-permute-start.3 = (bf16[512,256]{1,0:T(8,128)(2,1)S(1)}, bf16[512,256]{1,0:T(8,128)(2,1)S(1)}, u32[]{:S(2)}, u32[]{:S(2)}) collective-permute-start(bf16[512,256]{1,0:T(8,128)(2,1)S(1)} %collective-permute-done.1.refs_2_), channel_id=1, source_target_pairs={{0,2},{1,3},{2,4},{3,5},{4,6},{5,7},{6,0},{7,1},{8,10},{9,11},{10,... | collective-permute-start | bytes 786440 | tf_op jit(solution)/shard_map/ppermute | solution.py:391
  157.5 16.9 %collective-permute-start.19 = (bf16[512,256]{1,0:T(8,128)(2,1)S(1)}, bf16[512,256]{1,0:T(8,128)(2,1)S(1)}, u32[]{:S(2)}, u32[]{:S(2)}) collective-permute-start(bf16[512,256]{1,0:T(8,128)(2,1)S(1)} %collective-permute-done.17.refs_2_), channel_id=1, source_target_pairs={{0,2},{1,3},{2,4},{3,5},{4,6},{5,7},{6,0},{7,1},{8,10},{9,11},{10,... | collective-permute-start | bytes 786440 | tf_op jit(solution)/shard_map/ppermute | solution.py:391
  163.1 16.9 %collective-permute-start.31 = (bf16[512,256]{1,0:T(8,128)(2,1)S(1)}, bf16[512,256]{1,0:T(8,128)(2,1)S(1)}, u32[]{:S(2)}, u32[]{:S(2)}) collective-permute-start(bf16[512,256]{1,0:T(8,128)(2,1)S(1)} %collective-permute-done.29.refs_2_), channel_id=1, source_target_pairs={{0,2},{1,3},{2,4},{3,5},{4,6},{5,7},{6,0},{7,1},{8,10},{9,11},{10,... | collective-permute-start | bytes 786440 | tf_op jit(solution)/shard_map/ppermute | solution.py:391
  168.7 16.9 %collective-permute-start.43 = (bf16[512,256]{1,0:T(8,128)(2,1)S(1)}, bf16[512,256]{1,0:T(8,128)(2,1)S(1)}, u32[]{:S(2)}, u32[]{:S(2)}) collective-permute-start(bf16[512,256]{1,0:T(8,128)(2,1)S(1)} %collective-permute-done.41.refs_2_), channel_id=1, source_target_pairs={{0,2},{1,3},{2,4},{3,5},{4,6},{5,7},{6,0},{7,1},{8,10},{9,11},{10,... | collective-permute-start | bytes 786440 | tf_op jit(solution)/shard_map/ppermute | solution.py:391
  174.3 16.9 %collective-permute-start.44 = (bf16[512,256]{1,0:T(8,128)(2,1)S(1)}, bf16[512,256]{1,0:T(8,128)(2,1)S(1)}, u32[]{:S(2)}, u32[]{:S(2)}) collective-permute-start(bf16[512,256]{1,0:T(8,128)(2,1)S(1)} %collective-permute-done.42.refs_3_), channel_id=1, source_target_pairs={{0,2},{1,3},{2,4},{3,5},{4,6},{5,7},{6,0},{7,1},{8,10},{9,11},{10,... | collective-permute-start | bytes 786440 | tf_op jit(solution)/shard_map/ppermute | solution.py:391
  180.0 18.7 %collective-permute-start.4 = (bf16[512,256]{1,0:T(8,128)(2,1)S(1)}, bf16[512,256]{1,0:T(8,128)(2,1)}, u32[]{:S(2)}, u32[]{:S(2)}) collective-permute-start(bf16[512,256]{1,0:T(8,128)(2,1)S(1)} %collective-permute-done.2.refs_3_), channel_id=1, source_target_pairs={{0,2},{1,3},{2,4},{3,5},{4,6},{5,7},{6,0},{7,1},{8,10},{9,11},{10,... | collective-permute-start | bytes 786440 | tf_op jit(solution)/shard_map/ppermute | solution.py:391
  185.6 17.0 %collective-permute-start.20 = (bf16[512,256]{1,0:T(8,128)(2,1)}, bf16[512,256]{1,0:T(8,128)(2,1)}, u32[]{:S(2)}, u32[]{:S(2)}) collective-permute-start(bf16[512,256]{1,0:T(8,128)(2,1)} %collective-permute-done.18.refs_3_), channel_id=1, source_target_pairs={{0,2},{1,3},{2,4},{3,5},{4,6},{5,7},{6,0},{7,1},{8,10},{9,11},{10,... | collective-permute-start | bytes 786440 | tf_op jit(solution)/shard_map/ppermute | solution.py:391
  191.2 16.9 %collective-permute-start.45 = (bf16[512,256]{1,0:T(8,128)(2,1)S(1)}, bf16[512,256]{1,0:T(8,128)(2,1)S(1)}, u32[]{:S(2)}, u32[]{:S(2)}) collective-permute-start(bf16[512,256]{1,0:T(8,128)(2,1)S(1)} %collective-permute-done.43.refs_4_), channel_id=1, source_target_pairs={{0,2},{1,3},{2,4},{3,5},{4,6},{5,7},{6,0},{7,1},{8,10},{9,11},{10,... | collective-permute-start | bytes 786440 | tf_op jit(solution)/shard_map/ppermute | solution.py:391
  191.2 22.4 %collective-permute-start.46 = (bf16[512,256]{1,0:T(8,128)(2,1)S(1)}, bf16[512,256]{1,0:T(8,128)(2,1)S(1)}, u32[]{:S(2)}, u32[]{:S(2)}) collective-permute-start(bf16[512,256]{1,0:T(8,128)(2,1)S(1)} %collective-permute-done.44.refs_5_), channel_id=1, source_target_pairs={{0,2},{1,3},{2,4},{3,5},{4,6},{5,7},{6,0},{7,1},{8,10},{9,11},{10,... | collective-permute-start | bytes 786440 | tf_op jit(solution)/shard_map/ppermute | solution.py:391
  198.7 21.7 %collective-permute-start.32 = (bf16[512,256]{1,0:T(8,128)(2,1)S(1)}, bf16[512,256]{1,0:T(8,128)(2,1)S(1)}, u32[]{:S(2)}, u32[]{:S(2)}) collective-permute-start(bf16[512,256]{1,0:T(8,128)(2,1)S(1)} %copy-done.48), channel_id=1, source_target_pairs={{0,2},{1,3},{2,4},{3,5},{4,6},{5,7},{6,0},{7,1},{8,10},{9,11},{10,... | collective-permute-start | bytes 786440 | tf_op jit(solution)/shard_map/ppermute | solution.py:391
  202.5 22.4 %collective-permute-start.21 = (bf16[512,256]{1,0:T(8,128)(2,1)S(1)}, bf16[512,256]{1,0:T(8,128)(2,1)S(1)}, u32[]{:S(2)}, u32[]{:S(2)}) collective-permute-start(bf16[512,256]{1,0:T(8,128)(2,1)S(1)} %copy-done.52), channel_id=1, source_target_pairs={{0,2},{1,3},{2,4},{3,5},{4,6},{5,7},{6,0},{7,1},{8,10},{9,11},{10,... | collective-permute-start | bytes 786440 | tf_op jit(solution)/shard_map/ppermute | solution.py:391
  208.0 22.5 %collective-permute-start.22 = (bf16[512,256]{1,0:T(8,128)(2,1)}, bf16[512,256]{1,0:T(8,128)(2,1)S(1)}, u32[]{:S(2)}, u32[]{:S(2)}) collective-permute-start(bf16[512,256]{1,0:T(8,128)(2,1)} %collective-permute-done.20.refs_5_), channel_id=1, source_target_pairs={{0,2},{1,3},{2,4},{3,5},{4,6},{5,7},{6,0},{7,1},{8,10},{9,11},{10,... | collective-permute-start | bytes 786440 | tf_op jit(solution)/shard_map/ppermute | solution.py:391
  213.7 62.1 %collective-permute-start.11 = (bf16[1024,1024]{1,0:T(8,128)(2,1)S(1)}, bf16[1024,1024]{1,0:T(8,128)(2,1)S(1)}, u32[]{:S(2)}, u32[]{:S(2)}) collective-permute-start(bf16[1024,1024]{1,0:T(8,128)(2,1)S(1)} %shard_map.80), channel_id=1, source_target_pairs={{0,16},{8,24},{16,0},{24,8},{1,17},{9,25},{17,1},{25,9},{2,18},{10... | collective-permute-start | bytes 6291464 | tf_op jit(solution)/shard_map/ppermute | solution.py:394
  220.4 45.5 %collective-permute-start.5 = (bf16[512,256]{1,0:T(8,128)(2,1)S(1)}, bf16[512,256]{1,0:T(8,128)(2,1)S(1)}, u32[]{:S(2)}, u32[]{:S(2)}) collective-permute-start(bf16[512,256]{1,0:T(8,128)(2,1)S(1)} %copy-done.44), channel_id=1, source_target_pairs={{0,2},{1,3},{2,4},{3,5},{4,6},{5,7},{6,0},{7,1},{8,10},{9,11},{10,... | collective-permute-start | bytes 786440 | tf_op jit(solution)/shard_map/ppermute | solution.py:391
  224.9 16.9 %collective-permute-start.33 = (bf16[512,256]{1,0:T(8,128)(2,1)S(1)}, bf16[512,256]{1,0:T(8,128)(2,1)S(1)}, u32[]{:S(2)}, u32[]{:S(2)}) collective-permute-start(bf16[512,256]{1,0:T(8,128)(2,1)S(1)} %copy-done.50), channel_id=1, source_target_pairs={{0,2},{1,3},{2,4},{3,5},{4,6},{5,7},{6,0},{7,1},{8,10},{9,11},{10,... | collective-permute-start | bytes 786440 | tf_op jit(solution)/shard_map/ppermute | solution.py:391
  230.5 36.0 %collective-permute-start.6 = (bf16[512,256]{1,0:T(8,128)(2,1)}, bf16[512,256]{1,0:T(8,128)(2,1)S(1)}, u32[]{:S(2)}, u32[]{:S(2)}) collective-permute-start(bf16[512,256]{1,0:T(8,128)(2,1)} %collective-permute-done.4.refs_5_), channel_id=1, source_target_pairs={{0,2},{1,3},{2,4},{3,5},{4,6},{5,7},{6,0},{7,1},{8,10},{9,11},{10,... | collective-permute-start | bytes 786440 | tf_op jit(solution)/shard_map/ppermute | solution.py:391
  230.5 21.4 %collective-permute-start.34 = (bf16[512,256]{1,0:T(8,128)(2,1)S(1)}, bf16[512,256]{1,0:T(8,128)(2,1)S(1)}, u32[]{:S(2)}, u32[]{:S(2)}) collective-permute-start(bf16[512,256]{1,0:T(8,128)(2,1)S(1)} %collective-permute-done.32.refs_5_), channel_id=1, source_target_pairs={{0,2},{1,3},{2,4},{3,5},{4,6},{5,7},{6,0},{7,1},{8,10},{9,11},{10,... | collective-permute-start | bytes 786440 | tf_op jit(solution)/shard_map/ppermute | solution.py:391
  241.7 41.0 %collective-permute-start.23 = (bf16[256,2048]{1,0:T(8,128)(2,1)}, bf16[256,2048]{1,0:T(8,128)(2,1)S(1)}, u32[]{:S(2)}, u32[]{:S(2)}) collective-permute-start(bf16[256,2048]{1,0:T(8,128)(2,1)} %get-tuple-element.84), channel_id=1, source_target_pairs={{0,8},{8,0},{16,24},{24,16},{1,9},{9,1},{17,25},{25,17},{2,10},{10... | collective-permute-start | bytes 3145736 | tf_op jit(solution)/shard_map/ppermute | solution.py:397
  261.0 23.5 %collective-permute-start.35 = (bf16[256,2048]{1,0:T(8,128)(2,1)}, bf16[256,2048]{1,0:T(8,128)(2,1)S(1)}, u32[]{:S(2)}, u32[]{:S(2)}) collective-permute-start(bf16[256,2048]{1,0:T(8,128)(2,1)} %get-tuple-element.92), channel_id=1, source_target_pairs={{0,8},{8,0},{16,24},{24,16},{1,9},{9,1},{17,25},{25,17},{2,10},{10... | collective-permute-start | bytes 3145736 | tf_op jit(solution)/shard_map/ppermute | solution.py:397
  265.9 19.5 %collective-permute-start.47 = (bf16[256,2048]{1,0:T(8,128)(2,1)S(1)}, bf16[256,2048]{1,0:T(8,128)(2,1)S(1)}, u32[]{:S(2)}, u32[]{:S(2)}) collective-permute-start(bf16[256,2048]{1,0:T(8,128)(2,1)S(1)} %get-tuple-element.102), channel_id=1, source_target_pairs={{0,8},{8,0},{16,24},{24,16},{1,9},{9,1},{17,25},{25,17},{2,10},{10... | collective-permute-start | bytes 3145736 | tf_op jit(solution)/shard_map/ppermute | solution.py:397
  281.2 25.6 %collective-permute-start.12 = (bf16[4,128,1024]{2,1,0:T(8,128)(2,1)S(1)}, bf16[4,128,1024]{2,1,0:T(8,128)(2,1)S(1)}, u32[]{:S(2)}, u32[]{:S(2)}) collective-permute-start(bf16[4,128,1024]{2,1,0:T(8,128)(2,1)S(1)} %get-tuple-element.76), channel_id=1, source_target_pairs={{0,1},{1,0},{2,3},{3,2},{4,5},{5,4},{6,7},{7,6},{8,9},{9,8},{10,11... | collective-permute-start | bytes 3145736 | tf_op jit(solution)/shard_map/ppermute | solution.py:388
  284.9 24.2 %collective-permute-start.36 = (bf16[128,2048]{1,0:T(8,128)(2,1)S(1)}, bf16[128,2048]{1,0:T(8,128)(2,1)S(1)}, u32[]{:S(2)}, u32[]{:S(2)}) collective-permute-start(bf16[128,2048]{1,0:T(8,128)(2,1)S(1)} %shard_map.87), channel_id=1, source_target_pairs={{0,16},{8,24},{16,0},{24,8},{1,17},{9,25},{17,1},{25,9},{2,18},{10... | collective-permute-start | bytes 1572872 | tf_op jit(solution)/shard_map/ppermute | solution.py:394
  285.8 34.6 %collective-permute-start.48 = (bf16[128,2048]{1,0:T(8,128)(2,1)S(1)}, bf16[128,2048]{1,0:T(8,128)(2,1)S(1)}, u32[]{:S(2)}, u32[]{:S(2)}) collective-permute-start(bf16[128,2048]{1,0:T(8,128)(2,1)S(1)} %shard_map.91), channel_id=1, source_target_pairs={{0,16},{8,24},{16,0},{24,8},{1,17},{9,25},{17,1},{25,9},{2,18},{10... | collective-permute-start | bytes 1572872 | tf_op jit(solution)/shard_map/ppermute | solution.py:394
  287.6 43.2 %collective-permute-start.9 = (bf16[128,2048]{1,0:T(8,128)(2,1)S(1)}, bf16[128,2048]{1,0:T(8,128)(2,1)S(1)}, u32[]{:S(2)}, u32[]{:S(2)}) collective-permute-start(bf16[128,2048]{1,0:T(8,128)(2,1)S(1)} %shard_map.78), channel_id=1, source_target_pairs={{0,16},{8,24},{16,0},{24,8},{1,17},{9,25},{17,1},{25,9},{2,18},{10... | collective-permute-start | bytes 1572872 | tf_op jit(solution)/shard_map/ppermute | solution.py:394
  307.6 23.2 %collective-permute-start.25 = (bf16[32,2048]{1,0:T(8,128)(2,1)S(1)}, bf16[32,2048]{1,0:T(8,128)(2,1)S(1)}, u32[]{:S(2)}, u32[]{:S(2)}) collective-permute-start(bf16[32,2048]{1,0:T(8,128)(2,1)S(1)} %get-tuple-element.86), channel_id=1, source_target_pairs={{0,2},{1,3},{2,4},{3,5},{4,6},{5,7},{6,0},{7,1},{8,10},{9,11},{10,... | collective-permute-start | bytes 393224 | tf_op jit(solution)/shard_map/ppermute | solution.py:391
  309.9 23.2 %collective-permute-start.37 = (bf16[32,2048]{1,0:T(8,128)(2,1)S(1)}, bf16[32,2048]{1,0:T(8,128)(2,1)S(1)}, u32[]{:S(2)}, u32[]{:S(2)}) collective-permute-start(bf16[32,2048]{1,0:T(8,128)(2,1)S(1)} %get-tuple-element.94), channel_id=1, source_target_pairs={{0,2},{1,3},{2,4},{3,5},{4,6},{5,7},{6,0},{7,1},{8,10},{9,11},{10,... | collective-permute-start | bytes 393224 | tf_op jit(solution)/shard_map/ppermute | solution.py:391
  310.0 24.7 %collective-permute-start.38 = (bf16[32,2048]{1,0:T(8,128)(2,1)S(1)}, bf16[32,2048]{1,0:T(8,128)(2,1)S(1)}, u32[]{:S(2)}, u32[]{:S(2)}) collective-permute-start(bf16[32,2048]{1,0:T(8,128)(2,1)S(1)} %get-tuple-element.95), channel_id=1, source_target_pairs={{0,4},{1,5},{2,6},{3,7},{4,0},{5,1},{6,2},{7,3},{8,12},{9,13},{10,... | collective-permute-start | bytes 393224 | tf_op jit(solution)/shard_map/ppermute | solution.py:391
  334.7 25.5 %collective-permute-start.26 = (bf16[32,2048]{1,0:T(8,128)(2,1)S(1)}, bf16[32,2048]{1,0:T(8,128)(2,1)S(1)}, u32[]{:S(2)}, u32[]{:S(2)}) collective-permute-start(bf16[32,2048]{1,0:T(8,128)(2,1)S(1)} %get-tuple-element.87), channel_id=1, source_target_pairs={{0,4},{1,5},{2,6},{3,7},{4,0},{5,1},{6,2},{7,3},{8,12},{9,13},{10,... | collective-permute-start | bytes 393224 | tf_op jit(solution)/shard_map/ppermute | solution.py:391
  336.7 23.6 %collective-permute-start.27 = (bf16[32,2048]{1,0:T(8,128)(2,1)S(1)}, bf16[32,2048]{1,0:T(8,128)(2,1)S(1)}, u32[]{:S(2)}, u32[]{:S(2)}) collective-permute-start(bf16[32,2048]{1,0:T(8,128)(2,1)S(1)} %get-tuple-element.88), channel_id=1, source_target_pairs={{0,6},{1,7},{2,0},{3,1},{4,2},{5,3},{6,4},{7,5},{8,14},{9,15},{10,... | collective-permute-start | bytes 393224 | tf_op jit(solution)/shard_map/ppermute | solution.py:391
  339.0 24.0 %collective-permute-start.13 = (bf16[32,2048]{1,0:T(8,128)(2,1)S(1)}, bf16[32,2048]{1,0:T(8,128)(2,1)S(1)}, u32[]{:S(2)}, u32[]{:S(2)}) collective-permute-start(bf16[32,2048]{1,0:T(8,128)(2,1)S(1)} %get-tuple-element.78), channel_id=1, source_target_pairs={{0,2},{1,3},{2,4},{3,5},{4,6},{5,7},{6,0},{7,1},{8,10},{9,11},{10,... | collective-permute-start | bytes 393224 | tf_op jit(solution)/shard_map/ppermute | solution.py:391
  344.5 18.5 %collective-permute-start.14 = (bf16[32,2048]{1,0:T(8,128)(2,1)S(1)}, bf16[32,2048]{1,0:T(8,128)(2,1)S(1)}, u32[]{:S(2)}, u32[]{:S(2)}) collective-permute-start(bf16[32,2048]{1,0:T(8,128)(2,1)S(1)} %get-tuple-element.79), channel_id=1, source_target_pairs={{0,4},{1,5},{2,6},{3,7},{4,0},{5,1},{6,2},{7,3},{8,12},{9,13},{10,... | collective-permute-start | bytes 393224 | tf_op jit(solution)/shard_map/ppermute | solution.py:391
  369.4 18.2 %collective-permute-start.83 = (bf16[32,2048]{1,0:T(8,128)(2,1)S(1)}, bf16[32,2048]{1,0:T(8,128)(2,1)S(1)}, u32[]{:S(2)}, u32[]{:S(2)}) collective-permute-start(bf16[32,2048]{1,0:T(8,128)(2,1)S(1)} %get-tuple-element.133), channel_id=1, source_target_pairs={{0,4},{1,5},{2,6},{3,7},{4,0},{5,1},{6,2},{7,3},{8,12},{9,13},{10,... | collective-permute-start | bytes 393224 | tf_op jit(solution)/shard_map/ppermute | solution.py:391
  372.3 17.7 %collective-permute-start.84 = (bf16[32,2048]{1,0:T(8,128)(2,1)S(1)}, bf16[32,2048]{1,0:T(8,128)(2,1)S(1)}, u32[]{:S(2)}, u32[]{:S(2)}) collective-permute-start(bf16[32,2048]{1,0:T(8,128)(2,1)S(1)} %get-tuple-element.134), channel_id=1, source_target_pairs={{0,6},{1,7},{2,0},{3,1},{4,2},{5,3},{6,4},{7,5},{8,14},{9,15},{10,... | collective-permute-start | bytes 393224 | tf_op jit(solution)/shard_map/ppermute | solution.py:391
  374.1 25.4 %collective-permute-start.63 = (bf16[32,2048]{1,0:T(8,128)(2,1)S(1)}, bf16[32,2048]{1,0:T(8,128)(2,1)S(1)}, u32[]{:S(2)}, u32[]{:S(2)}) collective-permute-start(bf16[32,2048]{1,0:T(8,128)(2,1)S(1)} %get-tuple-element.121), channel_id=1, source_target_pairs={{0,4},{1,5},{2,6},{3,7},{4,0},{5,1},{6,2},{7,3},{8,12},{9,13},{10,... | collective-permute-start | bytes 393224 | tf_op jit(solution)/shard_map/ppermute | solution.py:391
  376.9 23.2 %collective-permute-start.64 = (bf16[32,2048]{1,0:T(8,128)(2,1)S(1)}, bf16[32,2048]{1,0:T(8,128)(2,1)S(1)}, u32[]{:S(2)}, u32[]{:S(2)}) collective-permute-start(bf16[32,2048]{1,0:T(8,128)(2,1)S(1)} %get-tuple-element.122), channel_id=1, source_target_pairs={{0,6},{1,7},{2,0},{3,1},{4,2},{5,3},{6,4},{7,5},{8,14},{9,15},{10,... | collective-permute-start | bytes 393224 | tf_op jit(solution)/shard_map/ppermute | solution.py:391
  379.7 22.0 %collective-permute-start.72 = (bf16[32,2048]{1,0:T(8,128)(2,1)S(1)}, bf16[32,2048]{1,0:T(8,128)(2,1)S(1)}, u32[]{:S(2)}, u32[]{:S(2)}) collective-permute-start(bf16[32,2048]{1,0:T(8,128)(2,1)S(1)} %get-tuple-element.126), channel_id=1, source_target_pairs={{0,2},{1,3},{2,4},{3,5},{4,6},{5,7},{6,0},{7,1},{8,10},{9,11},{10,... | collective-permute-start | bytes 393224 | tf_op jit(solution)/shard_map/ppermute | solution.py:391
  451.4 21.0 %collective-permute-start.55 = (bf16[4,32,1024]{2,1,0:T(8,128)(2,1)S(1)}, bf16[4,32,1024]{2,1,0:T(8,128)(2,1)}, u32[]{:S(2)}, u32[]{:S(2)}) collective-permute-start(bf16[4,32,1024]{2,1,0:T(8,128)(2,1)S(1)} %get-tuple-element.117.refs_0_), channel_id=1, source_target_pairs={{0,8},{8,0},{16,24},{24,16},{1,9},{9,1},{17,25},{25,17},{2,10},{10... | collective-permute-start | bytes 786440 | tf_op jit(solution)/shard_map/ppermute | solution.py:397
  452.6 16.8 %collective-permute-start.71 = (bf16[4,32,1024]{2,1,0:T(8,128)(2,1)}, bf16[4,32,1024]{2,1,0:T(8,128)(2,1)}, u32[]{:S(2)}, u32[]{:S(2)}) collective-permute-start(bf16[4,32,1024]{2,1,0:T(8,128)(2,1)} %collective-permute-done.70.refs_6_), channel_id=1, source_target_pairs={{0,8},{8,0},{16,24},{24,16},{1,9},{9,1},{17,25},{25,17},{2,10},{10... | collective-permute-start | bytes 786440 | tf_op jit(solution)/shard_map/ppermute | solution.py:397
  (99 other events, 1221.9 us)
